TPU v7x, 32 devices: a 4x4x1 block of a 4x4x8 slice. The times are simulated.
32 devices in a mesh: dp: 1 (over z), tp: 4 (over y), cp: 8 (over x, core).
Axes of the slice: x: 4, y: 4, z: 1, core: 2. Of those that a mesh axis runs over, the one named last changes fastest.
The devices are a block of a 4x4x8 slice.
Arguments:
- hidden: bfloat16 [8192, 3840], P(('dp', 'cp'))
- positions: int32 [8192], P(('dp', 'cp'))
- w_q: bfloat16 [2, 3840, 4096], P(None, None, 'tp')
- w_k: bfloat16 [2, 3840, 2048], P(None, None, 'tp')
- w_v: bfloat16 [2, 3840, 2048], P(None, None, 'tp')
- w_o: bfloat16 [2, 4096, 3840], P(None, 'tp')
- w_gate: bfloat16 [2, 3840, 15360], P(None, None, 'tp')
- w_up: bfloat16 [2, 3840, 15360], P(None, None, 'tp')
- w_down: bfloat16 [2, 15360, 3840], P(None, 'tp')
- norm_gain: float32 [2, 4, 3840], replicated
- qk_gain: float32 [2, 2, 256], replicated
Outputs:
- output 1: bfloat16 [8192, 3840], P(('dp', 'cp'))
- output 2: bfloat16 [2, 8192, 8, 256], P(None, ('dp', 'cp'), 'tp')
- output 3: bfloat16 [2, 8192, 8, 256], P(None, ('dp', 'cp'), 'tp')
All inputs are finite; a program needn't handle non-finite values.
Results may differ from a plain program's by a relative error of at most 0.0164515.
Values are sent between devices in bfloat16 or wider.
A program may use at most 768 MiB of HBM per device.

v0:
```python
import math
import jax
import jax.numpy as jnp
from jax import lax
from jax.sharding import PartitionSpec as P

WINDOW = 1024
THETAS = (10000.0, 1000000.0)
EPS = 1e-6
NEG_BIG = -1e30


def rms_scale(values, gain):
    mean_sq = jnp.mean(values * values, axis=-1, keepdims=True)
    return values * lax.rsqrt(mean_sq + EPS) * (1.0 + gain)


def rotary(values, positions, theta):
    head_dim = values.shape[-1]
    half_dim = head_dim // 2
    inv_freq = theta ** (-(jnp.arange(half_dim, dtype=jnp.float32) * 2.0) / head_dim)
    angles = positions.astype(jnp.float32)[..., None] * inv_freq
    cosine = jnp.cos(angles)[..., None, :]
    sine_val = jnp.sin(angles)[..., None, :]
    lower_half = values[..., :half_dim]
    upper_half = values[..., half_dim:]
    return jnp.concatenate([lower_half * cosine - upper_half * sine_val, upper_half * cosine + lower_half * sine_val], axis=-1)


def project_qkv(state_f, positions, w_q, w_k, w_v, layer_gain, qk_pair, theta, head_dim):
    normed = rms_scale(state_f, layer_gain[0]).astype(jnp.bfloat16)
    head_shape = normed.shape[:-1] + (-1, head_dim)
    q_proj = jnp.dot(normed, w_q, preferred_element_type=jnp.float32).reshape(head_shape)
    k_proj = jnp.dot(normed, w_k, preferred_element_type=jnp.float32).reshape(head_shape)
    v_rows = jnp.dot(normed, w_v, preferred_element_type=jnp.float32).astype(jnp.bfloat16).reshape(head_shape)
    q_rot = rotary(rms_scale(q_proj, qk_pair[0]), positions, theta).astype(jnp.bfloat16)
    k_rot = rotary(rms_scale(k_proj, qk_pair[1]), positions, theta).astype(jnp.bfloat16)
    return q_rot, k_rot, v_rows


def attend(queries, key_rows, val_rows, q_start, k_start, window, lo_block, hi_block, block_len):
    n_query, kv_local, groups, head_dim = queries.shape
    score_scale = head_dim ** -0.5
    query_index = q_start + jnp.arange(n_query)
    init_state = (
        jnp.full((kv_local, groups, n_query, 1), NEG_BIG, jnp.float32),
        jnp.zeros((kv_local, groups, n_query, 1), jnp.float32),
        jnp.zeros((kv_local, groups, n_query, head_dim), jnp.float32),
    )

    def loop_body(step_id, loop_state):
        run_max, run_sum, acc_out = loop_state
        key_blk = lax.dynamic_slice_in_dim(key_rows, step_id * block_len, block_len, 0)
        val_blk = lax.dynamic_slice_in_dim(val_rows, step_id * block_len, block_len, 0)
        scores = jnp.einsum('qhgd,uhd->hgqu', queries, key_blk, preferred_element_type=jnp.float32) * score_scale
        key_index = k_start + step_id * block_len + jnp.arange(block_len)
        distance = query_index[:, None] - key_index[None, :]
        allowed = (distance >= 0) & (distance < window) & (key_index >= 0)[None, :]
        scores = jnp.where(allowed, scores, NEG_BIG)
        new_max = jnp.maximum(run_max, jnp.max(scores, axis=-1, keepdims=True))
        prob_blk = jnp.exp(scores - new_max)
        factor = jnp.exp(run_max - new_max)
        run_sum = run_sum * factor + jnp.sum(prob_blk, axis=-1, keepdims=True)
        acc_out = acc_out * factor + jnp.einsum('hgqu,uhd->hgqd', prob_blk.astype(jnp.bfloat16), val_blk, preferred_element_type=jnp.float32)
        return new_max, run_sum, acc_out

    run_max, run_sum, acc_out = lax.fori_loop(lo_block, hi_block, loop_body, init_state)
    result = (acc_out / run_sum).astype(jnp.bfloat16)
    return jnp.transpose(result, (2, 0, 1, 3)).reshape(n_query, kv_local * groups * head_dim)


def finish_layer(state_f, attn_rows, w_o, w_gate, w_up, w_down, layer_gain):
    attn_out = lax.psum(jnp.dot(attn_rows, w_o, preferred_element_type=jnp.float32), 'tp')
    resid_f = (state_f + rms_scale(attn_out, layer_gain[1])).astype(jnp.bfloat16).astype(jnp.float32)
    normed = rms_scale(resid_f, layer_gain[2]).astype(jnp.bfloat16)
    gate_proj = jnp.dot(normed, w_gate, preferred_element_type=jnp.float32)
    up_proj = jnp.dot(normed, w_up, preferred_element_type=jnp.float32)
    act_rows = (jax.nn.gelu(gate_proj, approximate=True) * up_proj).astype(jnp.bfloat16)
    mlp_out = lax.psum(jnp.dot(act_rows, w_down, preferred_element_type=jnp.float32), 'tp')
    return (resid_f + rms_scale(mlp_out, layer_gain[3])).astype(jnp.bfloat16)


def solution(mesh):
    cp_size = mesh.shape['cp']
    row_spec = P(('dp', 'cp'), None)
    col_spec = P(None, None, 'tp')
    row_w_spec = P(None, 'tp', None)
    cache_spec = P(None, ('dp', 'cp'), 'tp', None)

    def device_fn(hidden, positions, w_q, w_k, w_v, w_o, w_gate, w_up, w_down, norm_gain, qk_gain):
        tok_rows = hidden.shape[0]
        head_dim = qk_gain.shape[-1]
        kv_local = w_k.shape[-1] // head_dim
        groups = w_q.shape[-1] // w_k.shape[-1]
        block_len = math.gcd(tok_rows, 256)
        q_start = lax.axis_index('cp') * tok_rows
        hi_block = (q_start + tok_rows) // block_len
        state_f = hidden.astype(jnp.float32)
        new_hidden = hidden
        k_list = []
        v_list = []
        for layer_id in range(2):
            q_rot, k_rot, v_rows = project_qkv(state_f, positions, w_q[layer_id], w_k[layer_id], w_v[layer_id], norm_gain[layer_id], qk_gain[layer_id], THETAS[layer_id], head_dim)
            k_all = lax.all_gather(k_rot, 'cp', axis=0, tiled=True)
            v_all = lax.all_gather(v_rows, 'cp', axis=0, tiled=True)
            if layer_id == 0:
                window = WINDOW
                lo_block = jnp.maximum(q_start - (WINDOW - 1), 0) // block_len
            else:
                window = tok_rows * cp_size
                lo_block = jnp.zeros((), jnp.int32)
            q_group = q_rot.reshape(tok_rows, kv_local, groups, head_dim)
            attn_rows = attend(q_group, k_all, v_all, q_start, 0, window, lo_block, hi_block, block_len)
            new_hidden = finish_layer(state_f, attn_rows, w_o[layer_id], w_gate[layer_id], w_up[layer_id], w_down[layer_id], norm_gain[layer_id])
            state_f = new_hidden.astype(jnp.float32)
            k_list.append(k_rot)
            v_list.append(v_rows)
        return new_hidden, jnp.stack(k_list), jnp.stack(v_list)

    return jax.shard_map(
        device_fn,
        mesh=mesh,
        in_specs=(row_spec, P(('dp', 'cp')), col_spec, col_spec, col_spec, row_w_spec, col_spec, col_spec, row_w_spec, P(), P()),
        out_specs=(row_spec, cache_spec, cache_spec),
        check_vma=False,
    )
```

profile of v0, /device:TPU:97, one launch (start us, length us, event | category | flops | bytes accessed | tf_op | source)
XLA Modules:
  0.0 2021.5 jit_solution(17394778709795847075)
XLA Ops:
  51.5 11.3 slice_bitcast_fusion
  62.8 10.4 copy.34
  73.2 13.2 multiply_reduce_fusion.5
  92.1 48.8 %all-gather.7.cloned.1.call-done = bf16[8192,2,256]{2,0,1:T(8,128)(2,1)} async-done(((bf16[1024,2,256]{2,0,1:T(8,128)(2,1)}), bf16[8192,2,256]{2,0,1:T(8,128)(2,1)}) %all-gather.7.cloned.1.call-update) | async-done | bytes 8388624 | tf_op jit(solution)/shard_map/all_gather | solution.py:105
  143.4 64.8 %while.30 = (s32[]{:T(128)}, f32[2,2,1024,1]{2,1,0,3:T(2,128)S(1)}, f32[2,2,1024,1]{2,1,0,3:T(2,128)S(1)}, f32[2,2,1024,256]{3,2,1,0:T(8,128)}, s32[]{:T(128)}, ...) while((s32[]{:T(128)}, f32[2,2,1024,1]{2,1,0,3:T(2,128)S(1)}, ...), condition=%wide.region_6.7_spmd.clone, body=%wide.region_3.6_spmd.clone.sunk | while | flops 1088698112 | bytes 58469108 | solution.py:67
  216.4 15.2 fusion.106
  231.7 273.2 %all-reduce.5.cloned.1.call-done = f32[1024,3840]{1,0:T(8,128)} async-done(((f32[1024,3840]{1,0:T(8,128)}), f32[1024,3840]{1,0:T(8,128)}) %all-reduce.5.cloned.1.call-update) | async-done | bytes 15728656 | tf_op jit(solution)/shard_map/psum | solution.py:73
  520.9 39.4 %fusion.54 = f32[1024,3840]{1,0:T(8,128)} fusion(bf16[2,3840,3840]{2,1,0:T(8,128)(2,1)} %param.21, bf16[1024,3840]{1,0:T(8,128)(2,1)S(1)} %get-tuple-element.244, f32[3840]{0:T(1024)S(1)} %get-tuple-element.195, f32[1024]{0:T(1024)S(1)} %add_rsqrt_fusion.9), kind=kOutput, calls=%fused_computation.72 | convolution fusion | flops 30214717440 | bytes 53103616 | tf_op jit(solution)/shard_map/dot_general | solution.py:76
  560.4 39.5 %fusion.78 = bf16[1024,3840]{1,0:T(8,128)(2,1)} fusion(f32[1024,3840]{1,0:T(8,128)} %fusion.54, bf16[2,3840,3840]{2,1,0:T(8,128)(2,1)} %param.22, bf16[1024,3840]{1,0:T(8,128)(2,1)S(1)} %get-tuple-element.244, f32[3840]{0:T(1024)S(1)} %get-tuple-element.195, f32[1024]{0:T(1024)S(1)} %add_rsqrt_fusion.9), kind=kOutput, calls=%fused_computation.110 | convolution fusion | flops 30254039040 | bytes 60967936 | tf_op jit(solution)/shard_map/dot_general | solution.py:77
  599.8 38.3 %fusion.50 = f32[1024,3840]{1,0:T(8,128)} fusion(bf16[1024,3840]{1,0:T(8,128)(2,1)} %fusion.78, bf16[2,3840,3840]{2,1,0:T(8,128)(2,1)} %param.23), kind=kOutput, calls=%fused_computation.68 | convolution fusion | flops 30198988800 | bytes 53084160 | tf_op jit(solution)/shard_map/dot_general | solution.py:79
  638.3 273.5 %all-reduce.7.cloned.1.call-done = f32[1024,3840]{1,0:T(8,128)} async-done(((f32[1024,3840]{1,0:T(8,128)}), f32[1024,3840]{1,0:T(8,128)}) %all-reduce.7.cloned.1.call-update) | async-done | bytes 15728656 | tf_op jit(solution)/shard_map/psum | solution.py:79
  927.9 9.5 fusion.127
  956.6 10.4 copy.41
  967.0 13.2 multiply_reduce_fusion.4
  986.5 49.2 %all-gather.9.cloned.1.call-done = bf16[8192,2,256]{0,2,1:T(8,128)(2,1)} async-done(((bf16[1024,2,256]{0,2,1:T(8,128)(2,1)}), bf16[8192,2,256]{0,2,1:T(8,128)(2,1)}) %all-gather.9.cloned.1.call-update) | async-done | bytes 8388624 | tf_op jit(solution)/shard_map/all_gather | solution.py:104
  1038.1 64.1 %while.31 = (s32[]{:T(128)}, f32[2,2,1024,1]{2,1,0,3:T(2,128)S(1)}, f32[2,2,1024,1]{2,1,0,3:T(2,128)S(1)}, f32[2,2,1024,256]{3,2,1,0:T(8,128)}, s32[]{:T(128)}, ...) while((s32[]{:T(128)}, f32[2,2,1024,1]{2,1,0,3:T(2,128)S(1)}, ...), condition=%wide.region_18.19_spmd.clone, body=%wide.region_15.18_spmd.clone.sunk | while | flops 1088698112 | bytes 58469108 | solution.py:67
  1110.4 15.1 fusion.100
  1126.1 463.9 %all-reduce.9.cloned.1.call-done = f32[1024,3840]{1,0:T(8,128)} async-done(((f32[1024,3840]{1,0:T(8,128)}), f32[1024,3840]{1,0:T(8,128)}) %all-reduce.9.cloned.1.call-update) | async-done | bytes 15728656 | tf_op jit(solution)/shard_map/psum | solution.py:73
  1596.5 9.5 fusion.83
  1606.1 39.4 %fusion.48 = f32[1024,3840]{1,0:T(8,128)} fusion(bf16[2,3840,3840]{2,1,0:T(8,128)(2,1)} %param.21, bf16[1024,3840]{1,0:T(8,128)(2,1)S(1)} %get-tuple-element.240, f32[3840]{0:T(1024)S(1)} %copy-done.22, f32[1024]{0:T(1024)S(1)} %add_rsqrt_fusion.5), kind=kOutput, calls=%fused_computation.66 | convolution fusion | flops 30214717440 | bytes 53103616 | tf_op jit(solution)/shard_map/dot_general | solution.py:76
  1645.5 39.3 %fusion.95 = bf16[1024,3840]{1,0:T(8,128)(2,1)} fusion(f32[1024,3840]{1,0:T(8,128)} %fusion.48, bf16[2,3840,3840]{2,1,0:T(8,128)(2,1)} %param.22, bf16[1024,3840]{1,0:T(8,128)(2,1)S(1)} %get-tuple-element.240, f32[3840]{0:T(1024)S(1)} %copy-done.22, f32[1024]{0:T(1024)S(1)} %add_rsqrt_fusion.5), kind=kOutput, calls=%fused_computation.127 | convolution fusion | flops 30254039040 | bytes 60967936 | tf_op jit(solution)/shard_map/dot_general | solution.py:77
  1684.8 38.1 %fusion.44 = f32[1024,3840]{1,0:T(8,128)} fusion(bf16[1024,3840]{1,0:T(8,128)(2,1)} %fusion.95, bf16[2,3840,3840]{2,1,0:T(8,128)(2,1)} %param.23), kind=kOutput, calls=%fused_computation.62 | convolution fusion | flops 30198988800 | bytes 53084160 | tf_op jit(solution)/shard_map/dot_general | solution.py:79
  1739.7 256.9 %all-reduce.11.cloned.1.call-done = f32[1024,3840]{1,0:T(8,128)} async-done(((f32[1024,3840]{1,0:T(8,128)}), f32[1024,3840]{1,0:T(8,128)}) %all-reduce.11.cloned.1.call-update) | async-done | bytes 15728656 | tf_op jit(solution)/shard_map/psum | solution.py:79
  2003.2 11.3 fusion.86
  (353 shorter events, 286.1 us)
Async XLA Ops:
  7.2 84.9 %all-gather.5.cloned.1.call-start = ((), (), s32[]{:S(2)}) async-start(), calls=%async_computation | async-start | bytes 9437184 | tf_op jit(solution)/shard_map/all_gather | solution.py:104
  24.4 8.3 copy-start.26
  24.4 8.9 copy-start.27
  40.7 100.2 %all-gather.7.cloned.1.call-start = ((), (), s32[]{:S(2)}) async-start(), calls=%async_computation.1 | async-start | bytes 9437184 | tf_op jit(solution)/shard_map/all_gather | solution.py:105
  49.5 13.2 copy-start.16
  51.0 453.9 %all-reduce.5.cloned.1.call-start = ((), (), s32[]{:S(2)}) async-start(), calls=%async_computation.2 | async-start | bytes 31457280 | tf_op jit(solution)/shard_map/psum | solution.py:73
  231.6 680.2 %all-reduce.7.cloned.1.call-start = ((), (), s32[]{:S(2)}) async-start(), calls=%async_computation.3 | async-start | bytes 31457280 | tf_op jit(solution)/shard_map/psum | solution.py:79
  520.9 39.4 %copy-start.6 = (bf16[1024,3840]{1,0:T(8,128)(2,1)}, bf16[1024,3840]{1,0:T(8,128)(2,1)S(1)}, u32[]{:S(2)}) copy-start(bf16[1024,3840]{1,0:T(8,128)(2,1)S(1)} %get-tuple-element.244) | copy-start | bytes 23592964
  638.2 280.2 %copy-start.21 = (f32[3840]{0:T(1024)S(1)}, f32[3840]{0:T(1024)}, u32[]{:S(2)}) copy-start(f32[3840]{0:T(1024)} %get-tuple-element.194) | copy-start | bytes 46084
  638.2 348.3 %all-gather.11.cloned.1.call-start = ((), (), s32[]{:S(2)}) async-start(), calls=%async_computation.5 | async-start | bytes 9437184 | tf_op jit(solution)/shard_map/all_gather | solution.py:105
  918.4 9.5 copy-start.23
  927.9 9.5 copy-start.4
  937.4 8.0 copy-start.18
  938.8 96.9 %all-gather.9.cloned.1.call-start = ((), (), s32[]{:S(2)}) async-start(), calls=%async_computation.4 | async-start | bytes 9437184 | tf_op jit(solution)/shard_map/all_gather | solution.py:104
  945.4 8.4 copy-start.25
  945.4 8.6 copy-start.8
  945.4 8.6 copy-start.9
  956.5 633.4 %all-reduce.9.cloned.1.call-start = ((), (), s32[]{:S(2)}) async-start(), calls=%async_computation.6 | async-start | bytes 31457280 | tf_op jit(solution)/shard_map/psum | solution.py:73
  967.0 13.2 copy-start.24
  1125.6 470.9 %copy-start.20 = (f32[3840]{0:T(1024)S(1)}, f32[3840]{0:T(1024)}, u32[]{:S(2)}) copy-start(f32[3840]{0:T(1024)} %get-tuple-element.192) | copy-start | bytes 46084
  1125.6 871.1 %all-reduce.11.cloned.1.call-start = ((), (), s32[]{:S(2)}) async-start(), calls=%async_computation.7 | async-start | bytes 31457280 | tf_op jit(solution)/shard_map/psum | solution.py:79
  1596.5 9.6 copy-start.22
  1606.0 39.4 %copy-start.5 = (bf16[1024,3840]{1,0:T(8,128)(2,1)}, bf16[1024,3840]{1,0:T(8,128)(2,1)S(1)}, u32[]{:S(2)}) copy-start(bf16[1024,3840]{1,0:T(8,128)(2,1)S(1)} %get-tuple-element.240) | copy-start | bytes 23592964
  1739.7 263.5 %copy-start.19 = (f32[3840]{0:T(1024)S(1)}, f32[3840]{0:T(1024)}, u32[]{:S(2)}) copy-start(f32[3840]{0:T(1024)} %get-tuple-element.191) | copy-start | bytes 46084
  (40 other events, 96.8 us)
Sparse Core Ops, SparseCore 0:
  40.8 51.2 all-gather.4
  93.7 47.1 all-gather.6
  231.7 273.0 all-reduce.4
  638.3 273.4 all-reduce.6
  938.9 47.5 all-gather.10
  988.5 47.1 all-gather.8
  1125.7 464.1 all-reduce.8
  1723.1 273.4 all-reduce.10
where the time goes:
time: 2030 us; the launch traced here: 2020 us
  waiting for transfers between devices  1370 us (67%)
  matrix products  412 us (20%)
  other arithmetic  123 us (6%)
  local copies, waits for them, and re-layouts  100 us (5%)
    psum x2, waiting for transfers between devices, finish_layer(): lax.psum(jnp.dot(attn_rows, w_o, preferred_element_type=jnp.float32), 'tp')  737 us
    psum x2, waiting for transfers between devices, finish_layer(): lax.psum(jnp.dot(act_rows, w_down, preferred_element_type=jnp.float32), '...  530 us
    dot_general x2, matrix products, finish_layer(): up_proj = jnp.dot(normed, w_up, preferred_element_type=jnp.float32)  78.8 us
    dot_general x2, matrix products, finish_layer(): gate_proj = jnp.dot(normed, w_gate, preferred_element_type=jnp.float32)  78.8 us
    dot_general x2, matrix products, finish_layer(): jnp.dot(act_rows, w_down, preferred_element_type=jnp.float32)  76.5 us
    reduce_sum x8, other arithmetic, rms_scale(): mean_sq = jnp.mean(values * values, axis=-1, keepdims=True)  59.8 us
    all_gather x2, waiting for transfers between devices, device_fn(): v_all = lax.all_gather(v_rows, 'cp', axis=0, tiled=True)  50.2 us
    all_gather x2, waiting for transfers between devices, device_fn(): k_all = lax.all_gather(k_rot, 'cp', axis=0, tiled=True)  50.1 us
  transfers between devices with their start and end apart: 8, of which 8 were waited for; matrix products, arithmetic and copies ran while one was open for 5% of the time, Pallas kernels for 0%

commit v1 on v0

v1 whole, which is shorter than its diff:
```python
import functools
import jax
import jax.numpy as jnp
from jax import lax
from jax.experimental import pallas as pl
from jax.experimental.pallas import tpu as pltpu
from jax.sharding import PartitionSpec as P

WINDOW = 1024
THETAS = (10000.0, 1000000.0)
EPS = 1e-6
NEG_BIG = -1e30
BF = jnp.bfloat16
F32 = jnp.float32
MESH = pl.DeviceIdType.MESH
ANY = pl.BlockSpec(memory_space=pl.ANY)
LOG2E = 1.4426950408889634
PAIR = 2
TWO = (0, 1)
TRIO = (0, 1, 2)
TILE = 256
LANES = 128
BIG_VMEM = 67_000_000
DMA = pltpu.SemaphoreType.DMA
VM = pltpu.VMEM


def span(start, size, unit=16):
    return pl.ds(pl.multiple_of(start, unit), size)


def send(src, dst, sent, received, to):
    return pltpu.make_async_remote_copy(src_ref=src, dst_ref=dst, send_sem=sent, recv_sem=received, device_id=to, device_id_type=MESH)


def each(method, *groups):
    for group in groups:
        for item in group:
            getattr(item, method)()


def start(*groups):
    each('start', *groups)


def wait(*groups):
    each('wait', *groups)


def arrived(*groups):
    each('wait_recv', *groups)


def departed(*groups):
    each('wait_send', *groups)


def greet(peers):
    barrier = pltpu.get_barrier_semaphore()
    for to in peers:
        pl.semaphore_signal(barrier, inc=1, device_id=to, device_id_type=MESH)
    pl.semaphore_wait(barrier, len(peers))


def around(axis, n, *distances):
    return [lax.rem(lax.axis_index(axis) + n + d, n) for d in distances]


def tp_peers(n_tp):
    return around('tp', n_tp, 1, -1, PAIR)


def cp_peers(n_cp):
    cp = lax.axis_index('cp')
    return (*around('cp', n_cp, PAIR, -PAIR, PAIR * PAIR), cp + 1 - PAIR * lax.rem(cp, PAIR))


def head_of(size):
    return pl.ds(0, size)


def on(axis, *devices):
    return [{axis: dev} for dev in devices]


def mean_scale(values):
    return lax.rsqrt(jnp.mean(values * values, axis=-1, keepdims=True) + EPS)


def rotate_heads(values, gain, cosine, sine):
    half = cosine.shape[-1]
    normed = values * mean_scale(values) * gain
    lower, upper = normed[:, :half], normed[:, half:]
    return jnp.concatenate([lower * cosine - upper * sine, upper * cosine + lower * sine], axis=-1).astype(BF)


def first_kernel(
    n_q, n_kv, n_tp, n_cp, strip, cut,
    x_ref, wk_ref, wv_ref, wq_ref, gain_ref, qg_ref, kg_ref, cos_ref, sin_ref, wo_hbm,
    o_hbm, kc_hbm, vc_hbm, wo_all, wo_next,
    h_ref, q_ref, kv_ref, past_ref,
    y1s, y1r, y2s, y2r, x1s, x1r, x2s, x2r, rs, rr, ks, kr, csem, osem,
):
    step = pl.program_id(0)
    rows = x_ref.shape[0]
    dim = qg_ref.shape[-1]
    o_rows = wo_hbm.shape[1]
    n_x = n_cp // PAIR
    shared = (o_rows // PAIR - n_x * strip) // PAIR

    me, cp = lax.axis_index('tp'), lax.axis_index('cp')
    core, chip = lax.rem(cp, PAIR), cp // PAIR
    right, left, opposite = tp_peers(n_tp)
    sides, sources = on('tp', right, left), (left, right, opposite)
    *ends, _, partner = on('cp', *cp_peers(n_cp))
    follow, prior = on('cp', *around('cp', n_cp, 1, -1))
    base = core * (o_rows // PAIR)

    def strip_of(distance):
        return base + PAIR * shared + lax.rem(chip + n_x + distance, n_x) * strip

    piece = o_rows // n_cp
    pieces = ((strip_of(0), strip, cut), (base, shared, shared // PAIR), (base + shared, shared, shared // PAIR), (cp * piece, piece, piece // PAIR))
    final = len(pieces) - 1

    def target(p):
        return wo_next if p == final else wo_all

    def y_first(p):
        at = span(*pieces[p][:PAIR])
        return [send(wo_hbm.at[p // final, at, :], target(p).at[me, at, :], y1s.at[p, d], y1r.at[p, d], sides[d]) for d in TWO]

    def halves(first, size, cut):
        return span(first, cut), span(first + cut, size - cut)

    def y_second(p):
        refs = [target(p).at[sources[d], halves(*pieces[p])[d], :] for d in TWO]
        return [send(refs[d], refs[d], y2s.at[p, d], y2r.at[p, d], sides[d]) for d in TWO]

    def x_first(s):
        ref = wo_all.at[sources[s], span(strip_of(0), strip), :]
        return [send(ref, ref, x1s.at[s, d], x1r.at[s, d], ends[d]) for d in TWO]

    def x_second(s):
        refs = [wo_all.at[sources[s], halves(strip_of((-1, 1)[d]), strip, cut)[d], :] for d in TWO]
        return [send(refs[d], refs[d], x2s.at[s, d], x2r.at[s, d], ends[d]) for d in TWO]

    def relay(kind, s):
        first, size = pieces[kind][:PAIR] if kind < final else (strip_of(kind - PAIR), strip)
        ref = wo_all.at[sources[s], span(first, size), :]
        return [send(ref, ref, rs.at[kind, s], rr.at[kind, s], partner)]

    def send_kv(t):
        return [send(kv_ref.at[t], past_ref.at[t], ks.at[t], kr.at[t], follow)]

    def keep_kv(t):
        return [pltpu.make_async_copy(kv_ref.at[t], (kc_hbm, vc_hbm)[t].at[0], csem.at[t])]

    group = n_q // n_kv

    def keep_o(h):
        some = pl.ds(h * group * dim, group * dim)
        return [pltpu.make_async_copy(q_ref.at[:, some], o_hbm.at[:, some], osem.at[h])]

    def y_stage(p, *more):
        arrived(y_first(p))
        start(y_second(p), *more, *[relay(p, s) for s in TWO if p < final])

    def x_stage(s):
        arrived(x_first(s))
        start(x_second(s), relay(final, s), relay(final + PAIR, s))

    def y_end(p):
        arrived(y_second(p))
        start(relay(p, PAIR), *([] if p else [x_first(PAIR)]))

    def x_end(s):
        arrived(x_second(s))
        start(relay(final + 1, s))

    q_step = PAIR * n_kv

    @pl.when(step == 0)
    def _():
        greet((*sides, *ends, follow, prior))
        start(*map(y_first, TWO))
        rb = 32

        @pl.loop(0, rows // rb)
        def _(i):
            at = span(i * rb, rb)
            xf = x_ref[at, :].astype(F32)
            h_ref[at, :] = (xf * mean_scale(xf) * gain_ref[...]).astype(BF)

    @pl.when(step == n_kv)
    def _():
        start(send_kv(0), keep_kv(0))

    @pl.when(step == q_step)
    def _():
        start(send_kv(1), keep_kv(1))
        y_stage(0, y_first(PAIR), *map(x_first, TWO))

    @pl.when(step == q_step + 3)
    def _():
        x_stage(0)

    def project(w_ref, store, finish):
        @pl.loop(0, rows // TILE)
        def _(i):
            at = span(i * TILE, TILE)
            store(at, finish(jnp.dot(h_ref[at, :], w_ref[0], preferred_element_type=F32), at))

    def into_kv(t, head):
        def store(at, value):
            kv_ref[t, at, span(head * dim, dim, LANES)] = value
        return store

    def into_q(at, value):
        q_ref[at, span((step - q_step) * dim, dim, LANES)] = value

    def rotate(gain_ref):
        return lambda a, at: rotate_heads(a, gain_ref[...], cos_ref[at, :], sin_ref[at, :])

    @pl.when(step < n_kv)
    def _():
        project(wk_ref, into_kv(0, step), rotate(kg_ref))

    @pl.when((step >= n_kv) & (step < q_step))
    def _():
        project(wv_ref, into_kv(1, step - n_kv), lambda a, at: a.astype(BF))

    @pl.when(step >= q_step)
    def _():
        project(wq_ref, into_q, rotate(qg_ref))

    def attend(h):
        head = slice(h * dim, (h + 1) * dim)
        for g in range(group):
            local_head(q_ref, h * group + g, *[ref.at[t, :, head] for t in TWO for ref in (past_ref, kv_ref)])
        start(keep_o(h))

    @pl.when(step == q_step + n_q - 1)
    def _():
        y_stage(1, y_first(final))
        y_end(0)
        x_stage(1)
        arrived(*map(send_kv, TWO))
        attend(0)
        x_end(0)
        y_stage(PAIR)
        x_stage(PAIR)
        y_stage(final)
        for h in range(1, n_kv):
            attend(h)
        x_end(1)
        y_end(1)
        y_end(PAIR)
        x_end(PAIR)
        arrived(y_second(final))
        departed(*map(send_kv, TWO))
        wait(*map(keep_kv, TWO), *map(keep_o, range(n_kv)))
        for s in TRIO:
            wait(*[relay(kind, s) for kind in range(PAIR * len(TRIO))])
            departed(x_first(s), x_second(s))
        for p in range(len(pieces)):
            departed(y_first(p), y_second(p))


def first_call(n_tp, n_cp, x, w_q, w_k, w_v, w_o, gain, q_gain, k_gain, cosine, sine):
    rows, width = x.shape
    dim = q_gain.shape[-1]
    n_q, n_kv = w_q.shape[-1] // dim, w_k.shape[-1] // dim
    at_k = lambda t: jnp.minimum(t, n_kv - 1)
    at_v = lambda t: jnp.clip(t - n_kv, 0, n_kv - 1)
    at_q = lambda t: jnp.maximum(t - PAIR * n_kv, 0)
    whole = lambda a: pl.BlockSpec(a.shape, lambda t: TWO[:1] * PAIR, pipeline_mode=pl.Buffered(1))
    w_spec = lambda at: pl.BlockSpec((1, width, dim), lambda t: (0, 0, at(t)))
    shape = lambda *sizes: jax.ShapeDtypeStruct(sizes, BF)
    q_width, kv_width = n_q * dim, n_kv * dim
    work = PAIR * width * (q_width + PAIR * kv_width)
    gathered, cache = shape(n_tp, *w_o.shape[1:]), shape(PAIR, rows, kv_width)
    return pl.pallas_call(
        functools.partial(first_kernel, n_q, n_kv, n_tp, n_cp, 80, 48),
        grid=(n_q + PAIR * n_kv,),
        in_specs=[whole(x), *map(w_spec, (at_k, at_v, at_q)), *map(whole, (gain, q_gain, k_gain, cosine, sine)), ANY],
        out_specs=[ANY] * 5,
        out_shape=[shape(rows, q_width), cache, cache, gathered, gathered],
        scratch_shapes=[VM((rows, width), BF), VM((rows, q_width), BF), VM(cache.shape, BF), VM(cache.shape, BF)]
        + [DMA((4, PAIR))] * 8 + [DMA((6, 3))] * PAIR + [DMA((PAIR,))] * 3 + [DMA((n_kv,))],
        compiler_params=pltpu.CompilerParams(dimension_semantics=("arbitrary",), collective_id=2, has_side_effects=True, vmem_limit_bytes=BIG_VMEM),
        cost_estimate=pl.CostEstimate(flops=rows * work, bytes_accessed=work, transcendentals=0),
        name="first",
    )(x, w_k, w_v, w_q, gain, q_gain, k_gain, cosine, sine, w_o)


def scores_of(q, k):
    return lax.dot_general(q, k, (((1,), (1,)), ((), ())), preferred_element_type=F32)


def local_head(q_ref, head, kp_ref, ko_ref, vp_ref, vo_ref):
    rows, dim = ko_ref.shape
    tile = TILE
    scale = dim ** -0.5 * LOG2E
    opening = lax.axis_index('cp') == 0
    row = lax.broadcasted_iota(jnp.int32, (tile, tile), 0)
    col = lax.broadcasted_iota(jnp.int32, (tile, tile), 1)
    for begin in range(0, rows, tile):
        end = begin + tile
        at = (slice(begin, end), slice(head * dim, (head + 1) * dim))
        q = q_ref[at]
        past = scores_of(q, kp_ref[begin:, :])
        here = scores_of(q, ko_ref[:end, :])
        past = jnp.concatenate([jnp.where(col > row, past[:, :tile], NEG_BIG), past[:, tile:]][:1 + (end < rows)], axis=1)
        past = jnp.where(opening, NEG_BIG, past)
        here = jnp.concatenate([here[:, :begin], jnp.where(col <= row, here[:, begin:], NEG_BIG)][begin == 0:], axis=1)
        top = jnp.maximum(*[jnp.max(a, axis=1, keepdims=True) for a in (past, here)])
        probs = [jnp.exp2((a - top) * scale) for a in (past, here)]
        total = sum(jnp.sum(p, axis=1, keepdims=True) for p in probs)
        acc = sum(jnp.dot(p.astype(BF), v, preferred_element_type=F32) for p, v in zip(probs, (vp_ref[begin:, :], vo_ref[:end, :])))
        q_ref[at] = (acc / total).astype(BF)


def fold_rows(values, op):
    return op(values.reshape(-1, 8, values.shape[-1]), axis=0)


def row_gather(n_tp, unit, gathered, own, s1, r1, s2, r2):
    sides = on('tp', *tp_peers(n_tp)[:PAIR])
    half = gathered.shape[-1] // PAIR
    seen = TRIO[::-PAIR]

    def first(u):
        at = span(u * unit, unit)
        return [send(own.at[at, :], gathered.at[seen[d], at, :], s1.at[u, d], r1.at[u, d], sides[d]) for d in TWO]

    def second(u):
        at = span(u * unit, unit)
        cols = [slice(d * half, (d + 1) * half) for d in TWO]
        return [send(gathered.at[seen[d], at, cols[d]], gathered.at[1, at, cols[d]], s2.at[u, d], r2.at[u, d], sides[d]) for d in TWO]

    return sides, first, second


def global_kernel(
    groups, n_tp, unit, q_ref, k_hbm, vt_hbm, o_hbm, og_hbm,
    k_ref, vt_ref, o_ref, m_ref, l_ref, ka_ref, kb_ref, xa_ref, xb_ref, acc_ref, sa_ref, sb_ref, pa_ref, pb_ref,
    ksem, vsem, osem, s1, r1, s2, r2,
):
    rows, width = q_ref.shape
    dim = acc_ref.shape[0]
    n_kv = k_hbm.shape[1] // dim
    block, wide = sa_ref.shape
    tile = wide // groups
    scale = dim ** -0.5 * LOG2E
    cp = lax.axis_index('cp')
    base = cp * (rows // block)
    last = base - 1
    sides, first, second = row_gather(n_tp, unit, og_hbm, o_ref, s1, r1, s2, r2)
    ready = tile // unit

    def load(b):
        at = span(b * rows, rows, LANES)
        return [pltpu.make_async_copy(k_hbm.at[at, :], k_ref.at[at, :], ksem.at[b]), pltpu.make_async_copy(vt_hbm.at[:, at], vt_ref.at[:, at], vsem.at[b])]

    def store(i):
        at = span(i * tile, tile)
        return [pltpu.make_async_copy(o_ref.at[at, :], o_hbm.at[at, :], osem.at[i])]

    @pl.loop(0, cp + 1)
    def _(b):
        start(load(cp - b))

    greet(sides)
    wait(load(cp))

    key = lax.broadcasted_iota(jnp.int32, (block, wide), 0)
    token = lax.rem(lax.broadcasted_iota(jnp.int32, (block, wide), 1), tile)

    @pl.loop(0, n_kv * (rows // tile))
    def _(turn):
        i, h = turn // n_kv, lax.rem(turn, n_kv)
        head = span(h * dim, dim, LANES)

        @pl.when(turn == 0)
        def _():
            @pl.loop(0, cp)
            def _(b):
                wait(load(b))

        q = jnp.concatenate([q_ref[span(i * tile, tile), span((h * groups + g) * dim, dim, LANES)] for g in range(groups)], axis=0)

        def score(b, s_ref, x_ref, masked=False):
            s = scores_of(k_ref[span(b * block, block), head], q)
            if masked:
                s = jnp.where(key <= token, s, NEG_BIG)
            s_ref[...] = s
            x_ref[...] = fold_rows(s, jnp.max)

        def soften(s_ref, x_ref, p_ref, keep_ref, opening=False):
            top = jnp.max(x_ref[...], axis=0, keepdims=True)
            if not opening:
                old = m_ref[...]
                top = jnp.maximum(old, top)
                keep_ref[...] = jnp.exp2((old - top) * scale)
            m_ref[...] = top
            prob = jnp.exp2((s_ref[...] - top) * scale)
            part = fold_rows(prob, jnp.sum)
            l_ref[...] = part if opening else l_ref[...] * keep_ref[...] + part
            p_ref[...] = prob.astype(BF)

        def weigh(b, p_ref, keep_ref, opening=False):
            part = jnp.dot(vt_ref[head, span(b * block, block, LANES)], p_ref[...], preferred_element_type=F32)
            acc_ref[...] = part if opening else acc_ref[...] * keep_ref[...] + part

        score(base + i, sa_ref, xa_ref, True)
        soften(sa_ref, xa_ref, pa_ref, ka_ref, True)
        weigh(base + i, pa_ref, ka_ref, True)

        @pl.loop(0, i)
        def _(b):
            score(base + b, sa_ref, xa_ref)
            soften(sa_ref, xa_ref, pa_ref, ka_ref)
            weigh(base + b, pa_ref, ka_ref)

        @pl.when(cp > 0)
        def _():
            score(jnp.int32(0), sa_ref, xa_ref)
            pb_ref[...] = jnp.zeros_like(pb_ref)
            kb_ref[...] = jnp.ones_like(kb_ref)

            @pl.loop(0, base // PAIR)
            def _(half):
                b = PAIR * half
                score(b + 1, sb_ref, xb_ref)
                soften(sa_ref, xa_ref, pa_ref, ka_ref)
                weigh(jnp.maximum(b - 1, 0), pb_ref, kb_ref)
                score(jnp.minimum(b + PAIR, last), sa_ref, xa_ref)
                soften(sb_ref, xb_ref, pb_ref, kb_ref)
                weigh(b, pa_ref, ka_ref)

            weigh(last, pb_ref, kb_ref)

        out = (acc_ref[...] / jnp.sum(l_ref[...], axis=0, keepdims=True)).T.astype(BF)
        for g in range(groups):
            o_ref[span(i * tile, tile), span((h * groups + g) * dim, dim, LANES)] = out[g * tile:(g + 1) * tile]

        @pl.when(turn == n_kv - 1)
        def _():
            start(store(0), *map(first, range(ready)))

        @pl.when(turn == n_kv)
        def _():
            for u in range(ready - 1):
                arrived(first(u))
                start(second(u))

    start(store(1))
    arrived(first(ready - 1))
    start(second(ready - 1))
    for u in range(ready):
        departed(first(u))
        wait(second(u))
    wait(*map(store, TWO))


def global_call(n_tp, q, k_all, vt_all, dim):
    rows, width = q.shape
    every, kv_width = k_all.shape
    groups = width // kv_width
    tile = rows // PAIR
    wide = groups * tile
    unit = LANES
    vmem = pl.BlockSpec(memory_space=VM)
    row, slab = VM((1, wide), F32), VM((8, wide), F32)
    return pl.pallas_call(
        functools.partial(global_kernel, groups, n_tp, unit),
        in_specs=[vmem, ANY, ANY],
        out_specs=[ANY, ANY],
        out_shape=[jax.ShapeDtypeStruct(q.shape, BF), jax.ShapeDtypeStruct((n_tp - 1, *q.shape), BF)],
        scratch_shapes=[VM(k_all.shape, BF), VM(vt_all.shape, BF), VM(q.shape, BF), row, slab, row, row, slab, slab, VM((dim, wide), F32)]
        + [VM((tile, wide), t) for t in (F32, F32, BF, BF)] + [DMA((every // rows,))] * PAIR + [DMA((PAIR,))] + [DMA((tile // unit, PAIR))] * 4,
        compiler_params=pltpu.CompilerParams(collective_id=3, has_side_effects=True, vmem_limit_bytes=BIG_VMEM),
        cost_estimate=pl.CostEstimate(flops=PAIR * rows * every * width, bytes_accessed=PAIR * every * width, transcendentals=0),
        name="attend_global",
    )(q, k_all, vt_all)


def block_kernel(layer, n_tp, n_cp, tm, nt, unit, ready, follow, *refs):
    queue = iter(refs)

    def take(names):
        return [ref for _, ref in zip(range(names), queue)]

    o_hbm, wo_own, wo_hbm, x_hbm, wg_hbm, wu_hbm, wd_hbm, gain_ref = take(8)
    if ready:
        take(1)
    if follow:
        wq_hbm, wk_hbm, wv_hbm, hg_ref, qg_ref, kg_ref, cos_ref, sin_ref, *_ = take(11)
    out_hbm, og_hbm = take(PAIR)
    if follow:
        q_hbm, ka_hbm, va_hbm, k_hbm, v_hbm, wn_hbm = take(6)
    wbuf, pbuf, r1, r2, xb, mbuf, sbuf, obuf, xbuf, rown, wsem, osem, xsem, stsem = take(14)
    o1s, o1r, o2s, o2r, s1s, s1r, sbs, sbr, sas, sar, g1s, g1r, g2s, g2r = take(14)
    if follow:
        nbuf, vbuf, nsem, fs, fr, hs, hr, ps, pr, a1s, a1r, a2s, a2r, bs, br_ = take(15)

    rows, width = x_hbm.shape
    o_width = o_hbm.shape[1]
    hidden = wd_hbm.shape[1]
    chunks = rows // tm
    fine = tm // unit
    br = unit // n_tp
    hw = width // PAIR
    units = rows // unit
    n_o, n_g, n_d = width // nt, hidden // nt, width // nt
    n_og = n_o + PAIR * n_g
    per = n_og + n_d
    depth, lag = 3, PAIR
    n_n = 0
    if follow:
        dim = qg_ref.shape[-1]
        nw = wk_hbm.shape[-1]
        n_qt = wq_hbm.shape[-1] // nw
        n_n = n_qt + PAIR
    total = chunks * per + (chunks + 1) * n_n

    me, cp = lax.axis_index('tp'), lax.axis_index('cp')
    right, left, opposite = tp_peers(n_tp)
    near = (right, left)
    far = (left, right)
    ahead, behind, across, mate = cp_peers(n_cp)
    *ends, partner = on('cp', ahead, behind, mate)
    sides, o_first, o_second = row_gather(n_tp, unit, og_hbm, o_hbm, o1s, o1r, o2s, o2r)

    def base_of(n):
        return n * per + jnp.maximum(n - lag, 0) * n_n

    def step_of(index):
        if not follow:
            return lax.rem(index, per)
        head, body = lag * per, (chunks - lag) * (per + n_n)
        late = index - head
        tail = per + lax.rem(jnp.maximum(late - body, 0), n_n)
        return jnp.where(late < 0, lax.rem(index, per), jnp.where(late < body, lax.rem(jnp.maximum(late, 0), per + n_n), tail))

    def columns(tile):
        return span(tile * nt, nt, LANES)

    def part_of(slot, length, first=0):
        return wbuf.at[slot, pl.ds(first, length), :]

    def narrow(slot):
        return wbuf.at[slot, head_of(width), head_of(nw)]

    def start_w(index):
        step, slot = step_of(index), lax.rem(index, depth)

        def load(wanted, src, dst, s=0):
            @pl.when((index < total) & wanted)
            def _():
                pltpu.make_async_copy(src, dst, wsem.at[slot, s]).start()

        for s in range(n_tp):
            src = wo_hbm.at[lax.rem(me + s, n_tp)] if s else wo_own.at[layer]
            load(step < n_o, src.at[:, columns(jnp.minimum(step, n_o - 1))], part_of(slot, o_width, s * o_width), s)
        middle = jnp.clip(step - n_o, 0, n_og - n_o - 1)
        for t, src in enumerate((wg_hbm, wu_hbm)):
            load((step >= n_o) & (step < n_og) & (lax.rem(middle, PAIR) == t), src.at[layer, :, columns(middle // PAIR)], part_of(slot, width))
        load((step >= n_og) & (step < per), wd_hbm.at[layer, :, columns(jnp.clip(step - n_og, 0, n_d - 1))], part_of(slot, hidden))
        if follow:
            for t, src in enumerate((wk_hbm, wv_hbm)):
                load(step == per + t, src.at[layer + 1], narrow(slot))
            late = step - per - PAIR
            load(late >= 0, wq_hbm.at[layer + 1, :, span(jnp.clip(late, 0, n_qt - 1) * nw, nw, LANES)], narrow(slot))

    def wait_w(index, length):
        slot = lax.rem(index, depth)
        pltpu.make_async_copy(wd_hbm.at[layer, head_of(length), columns(0)], part_of(slot, length), wsem.at[slot, 0]).wait()
        return slot

    def wait_wo(index):
        slot = lax.rem(index, depth)
        for s in range(n_tp):
            pltpu.make_async_copy(wo_own.at[layer, :, columns(0)], part_of(slot, o_width, s * o_width), wsem.at[slot, s]).wait()
        return slot

    def o_serve(u):
        arrived(o_first(u))
        start(o_second(u))

        @pl.when(u + PAIR < units)
        def _():
            start(o_first(u + PAIR))

    def o_finish(u):
        departed(o_first(u))
        wait(o_second(u))

    cols = [pl.ds(d * hw, hw) for d in TWO]
    other = cols[::-1]

    def partial(k):
        return pbuf.at[lax.rem(k // fine, PAIR)]

    def part(k, dev):
        return span(lax.rem(k, fine) * unit + dev * br, br)

    def reduce(kind, k, d, dev, side, dst):
        s_sem, r_sem = kind
        return [send(partial(k).at[part(k, dev), side], dst, s_sem.at[k, d], r_sem.at[k, d], sides[d])]

    def s_far(k, d):
        return reduce((s1s, s1r), k, d, opposite, cols[d], r1.at[k, d])

    def s_plain(k, d):
        return reduce((sbs, sbr), k, d, near[d], other[d], r2.at[k, d, :, other[d]])

    def s_sum(k, d):
        return reduce((sas, sar), k, d, near[d], cols[d], r2.at[k, d, :, cols[d]])

    def x_rows(k, dev):
        return span(k * unit + dev * br, br)

    def x_first(k):
        return [send(xb.at[k], out_hbm.at[x_rows(k, me), :], g1s.at[k, d], g1r.at[k, d], sides[d]) for d in TWO]

    def x_second(k):
        refs = [out_hbm.at[x_rows(k, far[d]), cols[d]] for d in TWO]
        return [send(refs[d], refs[d], g2s.at[k, d], g2r.at[k, d], sides[d]) for d in TWO]

    def x_own(k):
        return [pltpu.make_async_copy(xb.at[k], out_hbm.at[x_rows(k, me), :], stsem.at[k])]

    def e0(n):
        for kind in (s_far, s_plain):
            for i in range(fine):
                start(*[kind(n * fine + i, d) for d in TWO])

    def e1(k):
        p = partial(k)
        for d in TWO:
            at = (part(k, near[d]), cols[d])
            arrived(s_far(k, d))
            p[at] = p[at] + r1[k, d]
            start(s_sum(k, d))

    def e2(k):
        p = partial(k)
        for d in TWO:
            arrived(s_plain(k, d), s_sum(k, d))
        sub = 16
        for begin in range(0, br, sub):
            at = pl.ds(begin, sub)
            z = sum([r2[k, d, at, :] for d in TWO], p[span(lax.rem(k, fine) * unit + me * br + begin, sub), :])
            r = rown[lax.rem(k // fine, PAIR), lax.rem(k, fine), at, :].astype(F32)
            xb[k, at, :] = (r + z * mean_scale(z) * gain_ref[PAIR:, :]).astype(BF)
        start(x_first(k), x_own(k))
        for d in TWO:
            departed(s_far(k, d), s_plain(k, d), s_sum(k, d))

    def e3(k):
        arrived(x_first(k))
        start(x_second(k))

    def e4(k):
        wait(x_second(k), x_own(k))
        departed(x_first(k))

    def all_of(step, n):
        for i in range(fine):
            step(n * fine + i)

    def batch(n):
        return n, n * tm, tm

    ends_of = [(jnp.int32(chunks - 1 + i), jnp.int32(rows - tm + i * unit), unit) for i in TWO]

    def kv_at(c, dev, t):
        at = span(dev * rows + c[1], c[PAIR], LANES)
        return va_hbm.at[:, at] if t else ka_hbm.at[at, :]

    def kv_mine(c, t):
        slot, some = lax.rem(c[0], depth), head_of(c[PAIR])
        return vbuf.at[slot, :, some] if t else nbuf.at[slot, 0, some, :]

    def kv_first(c):
        return [send(kv_mine(c, t), kv_at(c, cp, t), fs.at[c[0], t, d], fr.at[c[0], t, d], to) for t in TWO for d, to in enumerate((*ends, partner))]

    def kv_second(c):
        refs = [kv_at(c, (behind, ahead)[d], d) for d in TWO]
        return [send(refs[d], refs[d], hs.at[c[0], d], hr.at[c[0], d], ends[d]) for d in TWO]

    def kv_relay(c, e):
        refs = [kv_at(c, (behind, ahead, across)[e], t) for t in TWO]
        return [send(refs[t], refs[t], ps.at[c[0], e, t], pr.at[c[0], e, t], partner) for t in TWO]

    def stores(c):
        k, first, size = c
        at, slot, some = span(first, size), lax.rem(k, depth), head_of(size)
        pairs = [(kv_mine(c, t), kv_at(c, cp, t)) for t in TWO] + [(nbuf.at[slot, t, some, :], (k_hbm, v_hbm)[t].at[1, at, :]) for t in TWO]
        pairs += [(nbuf.at[slot, PAIR + t, some, :], q_hbm.at[at, pl.ds(t * nw, nw)]) for t in range(n_qt)]
        return [pltpu.make_async_copy(src, dst, nsem.at[slot, t]) for t, (src, dst) in enumerate(pairs)]

    def f0(c, base):
        k, first, size = c
        at, slot, some = span(first, size), lax.rem(k, depth), head_of(size)
        load = [pltpu.make_async_copy(out_hbm.at[at, :], xbuf.at[some, :], xsem)]
        start(load)
        wait(load)
        sub = 32

        @pl.loop(0, size // sub)
        def _(i):
            rows_of = span(i * sub, sub)
            xf = xbuf[rows_of, :].astype(F32)
            mbuf[rows_of, :] = (xf * mean_scale(xf) * hg_ref[...]).astype(BF)

        cosine, sine = cos_ref[at, :], sin_ref[at, :]
        for t in range(n_n):
            start_w(base + t + PAIR)
            w_slot = lax.rem(base + t, depth)
            pltpu.make_async_copy(wk_hbm.at[layer + 1], narrow(w_slot), wsem.at[w_slot, 0]).wait()
            acc = jnp.dot(mbuf[some, :], narrow(w_slot)[...], preferred_element_type=F32)
            if t == 1:
                nbuf[slot, t, some, :] = acc.astype(BF)
                vbuf[slot, :, some] = acc.T.astype(BF)
                start(kv_first(c))
            else:
                for begin in range(0, nw, dim):
                    this = slice(begin, begin + dim)
                    nbuf[slot, t, some, this] = rotate_heads(acc[:, this], qg_ref[...] if t else kg_ref[...], cosine, sine)
        start(stores(c))

    def f1(c):
        arrived(kv_first(c))
        start(kv_second(c), *[kv_relay(c, e) for e in TWO])

    def f2(c):
        arrived(kv_second(c))
        start(kv_relay(c, PAIR))
        departed(kv_first(c))
        wait(stores(c))

    def f3(c):
        wait(*[kv_relay(c, e) for e in TRIO])
        departed(kv_second(c))

    piece = o_width // n_cp

    def strips(s, dev, size=piece, part=0):
        return wn_hbm.at[lax.rem(me + 1 + s, n_tp), span(dev * piece + part * size, size), :]

    def a_first(s):
        ref = strips(s, cp)
        return [send(ref, ref, a1s.at[s, d], a1r.at[s, d], ends[d]) for d in TWO]

    def a_second(s):
        refs = [strips(s, (behind, ahead)[d], piece // PAIR, d) for d in TWO]
        return [send(refs[d], refs[d], a2s.at[s, d], a2r.at[s, d], ends[d]) for d in TWO]

    def a_relay(s, *kinds):
        refs = {e: strips(s, (cp, behind, ahead, across)[e]) for e in kinds}
        return [send(ref, ref, bs.at[s, e], br_.at[s, e], partner) for e, ref in refs.items()]

    def a_serve(s):
        arrived(a_first(s))
        start(a_second(s), a_relay(s, *TRIO[1:]))

    def a_finish(s):
        arrived(a_second(s))
        start(a_relay(s, len(TRIO)))

    def a_drain(s):
        wait(a_relay(s, *TRIO, len(TRIO)))
        departed(a_first(s), a_second(s))

    for t in TWO:
        start_w(jnp.int32(t))
    greet((*sides, *ends, partner) if follow else sides)
    start(*[o_first(ready + t) for t in TWO])
    if follow:
        for s in TRIO:
            start(a_first(s), a_relay(s, 0))
    served = ready
    if not ready:
        for served in TWO:
            o_serve(served)
        served = PAIR

    def serve(n, place):
        if served + place < units:
            @pl.when(n == 0)
            def _():
                o_serve(served + place)

    def load_rows(n):
        at = span(n * tm, tm)
        copies = [pltpu.make_async_copy(x_hbm.at[at, :], xbuf, xsem)]
        for s in range(n_tp):
            src = og_hbm.at[s - 1] if s else o_hbm
            copies.append(pltpu.make_async_copy(src.at[at, :], obuf.at[:, pl.ds(s * o_width, o_width)], osem.at[s]))
        return copies

    def chunk(n, _):
        base = base_of(n)
        slot_p = lax.rem(n, PAIR)
        p = pbuf.at[slot_p]

        @pl.when(n * tm >= ready * unit)
        def _():
            all_of(o_finish, n)

        start(load_rows(n))
        wait(load_rows(n))

        @pl.loop(0, n_o)
        def _(j):
            start_w(base + j + PAIR)
            slot = wait_wo(base + j)
            p[:, columns(j)] = jnp.dot(obuf[...], wbuf[slot], preferred_element_type=F32)

            @pl.when(j == n_o // PAIR)
            def _():
                serve(n, 0)

        serve(n, 1)

        if follow:
            @pl.when(n > lag)
            def _():
                f1(batch(n - 1 - lag))

        sub = 32

        @pl.loop(0, tm // sub)
        def _(i):
            at = span(i * sub, sub)
            z = p[at, :]
            r = (xbuf[at, :].astype(F32) + z * mean_scale(z) * gain_ref[0:1, :]).astype(BF)
            xbuf[at, :] = r
            rf = r.astype(F32)
            mbuf[at, :] = (rf * mean_scale(rf) * gain_ref[1:2, :]).astype(BF)

        for i in range(fine):
            rown[slot_p, i] = xbuf[span(i * unit + me * br, br), :]

        @pl.loop(0, n_g)
        def _(j):
            index = base + n_o + PAIR * j
            start_w(index + PAIR)
            slot = wait_w(index, width)
            gate = jnp.dot(mbuf[...], part_of(slot, width)[...], preferred_element_type=F32)
            start_w(index + depth)
            slot = wait_w(index + 1, width)
            up = jnp.dot(mbuf[...], part_of(slot, width)[...], preferred_element_type=F32)
            sbuf[:, columns(j)] = (jax.nn.gelu(gate, approximate=True) * up).astype(BF)

            @pl.when((j == 0) & (n >= 1))
            def _():
                all_of(e1, n - 1)
                if follow:
                    a_serve(n - 1)

            @pl.when(j == 1)
            def _():
                serve(n, PAIR)

                @pl.when(n >= lag)
                def _():
                    all_of(e3, n - lag)

            @pl.when(j == depth)
            def _():
                serve(n, depth)

        @pl.when(n >= 1)
        def _():
            all_of(e2, n - 1)

        if follow:
            @pl.when(n > lag)
            def _():
                f2(batch(n - 1 - lag))

        @pl.loop(0, n_d)
        def _(j):
            index = base + n_og + j
            start_w(index + PAIR)
            slot = wait_w(index, hidden)
            p[:, columns(j)] = jnp.dot(sbuf[...], part_of(slot, hidden)[...], preferred_element_type=F32)

            @pl.when(j == 0)
            def _():
                serve(n, 4)

        serve(n, 5)
        e0(n)

        @pl.when(n >= lag)
        def _():
            all_of(e4, n - lag)
            if follow:
                f0(batch(n - lag), base + per)

        return 0

    lax.fori_loop(0, chunks, chunk, 0)
    every = [jnp.int32(k) for k in range(chunks)]
    tail = jnp.int32(total - depth * n_n)
    *_, before, last = every
    all_of(e1, last)
    all_of(e3, before)
    if follow:
        early, middle, *late = *map(batch, every[1:-1]), *ends_of
        f1(early)
    all_of(e2, last)
    all_of(e4, before)
    if follow:
        f2(early)
        f0(middle, tail)
    all_of(e3, last)
    if follow:
        each_strip = lambda step: [step(s) for s in TRIO]
        each_strip(a_finish)
        for i, c in enumerate(late):
            e4(last * fine + i)
            f0(c, tail + (1 + i) * n_n)
            (f2 if i else f1)(middle)
        for step in (f1, f2):
            for c in late:
                step(c)
        each_strip(a_drain)
        for c in (batch(every[0]), early, middle, *late):
            f3(c)
    else:
        all_of(e4, last)


def block_call(layer, n_tp, n_cp, o, w_o, wo_all, x, w_gate, w_up, w_down, gain, gathered=None, following=None):
    rows, width = x.shape
    o_width = o.shape[1]
    hidden = w_down.shape[1]
    tm, nt, unit = TILE, 768, LANES
    chunks, br, units = rows // tm, unit // n_tp, rows // unit
    vmem = pl.BlockSpec(memory_space=VM)
    deep = max(n_tp * o_width, width, hidden)
    shape = lambda *sizes: jax.ShapeDtypeStruct(sizes, BF)
    operands = [o, w_o, wo_all, x, w_gate, w_up, w_down, gain]
    in_specs = [ANY] * 7 + [vmem]
    out_shape = [shape(rows, width), shape(n_tp - 1, rows, o_width)]
    scratch = [
        VM((3, deep, nt), BF), VM((PAIR, tm, width), F32), VM((units, PAIR, br, width // PAIR), F32), VM((units, PAIR, br, width), F32),
        VM((units, br, width), BF), VM((tm, width), BF), VM((tm, hidden), BF), VM((tm, n_tp * o_width), BF), VM((tm, width), BF), VM((PAIR, tm // unit, br, width), BF),
        DMA((3, n_tp)), DMA((n_tp,)), DMA, DMA((units,)),
    ] + [DMA((units, PAIR))] * 14
    aliases = {}
    if gathered is not None:
        aliases[len(operands)] = 1
        operands.append(gathered)
        in_specs.append(ANY)
    if following is not None:
        q_width, kv_width = following[0].shape[-1], following[1].shape[-1]
        n_qt = q_width // kv_width
        operands += following
        in_specs += [ANY] * 3 + [vmem] * 5 + [ANY] * 3
        kept = following[-3:]
        out_shape += [shape(rows, q_width), shape(n_cp * rows, kv_width), shape(kv_width, n_cp * rows)] + [shape(*a.shape) for a in kept]
        aliases.update((len(operands) - i, len(out_shape) - i) for i in range(1, 1 + len(kept)))
        scratch += [VM((3, n_qt + PAIR, tm, kv_width), BF), VM((3, kv_width, tm), BF), DMA((3, n_qt + 4))]
        late = chunks + 1
        for count, sizes in ((1, (late, PAIR, 3)), (1, (late, PAIR)), (1, (late, 3, PAIR)), (PAIR, (n_tp - 1, PAIR)), (1, (n_tp - 1, 4))):
            scratch += [DMA(sizes)] * (PAIR * count)
    weights = width * (n_tp * o_width + 3 * hidden)
    return pl.pallas_call(
        functools.partial(block_kernel, layer, n_tp, n_cp, tm, nt, unit, 0 if gathered is None else units // PAIR, following is not None),
        in_specs=in_specs,
        out_specs=[ANY] * len(out_shape),
        out_shape=out_shape,
        scratch_shapes=scratch,
        input_output_aliases=aliases,
        compiler_params=pltpu.CompilerParams(collective_id=layer, has_side_effects=True, vmem_limit_bytes=BIG_VMEM),
        cost_estimate=pl.CostEstimate(flops=4 * rows * weights, bytes_accessed=8 * weights, transcendentals=0),
        name=f"block_{layer}",
    )(*operands)


def angles_of(positions, dim, theta):
    inv_freq = theta ** (-(jnp.arange(dim // 2, dtype=F32) * 2.0) / dim)
    angles = positions.astype(F32)[..., None] * inv_freq
    return jnp.cos(angles), jnp.sin(angles)


def solution(mesh):
    n_cp, n_tp = mesh.shape['cp'], mesh.shape['tp']
    row_spec = P(('dp', 'cp'), None)
    col_spec = P(None, None, 'tp')
    row_w_spec = P(None, 'tp', None)
    cache_spec = P(None, ('dp', 'cp'), 'tp', None)

    def device_fn(hidden, positions, w_q, w_k, w_v, w_o, w_gate, w_up, w_down, norm_gain, qk_gain):
        rows, width = hidden.shape
        dim = qk_gain.shape[-1]
        n_kv = w_k.shape[-1] // dim
        gains = 1.0 + norm_gain
        head_gains = 1.0 + qk_gain
        angles = [angles_of(positions, dim, theta) for theta in THETAS]
        norms = [(gains[l, :1], head_gains[l, :1], head_gains[l, 1:], *angles[l]) for l in TWO]
        o_0, k_cache, v_cache, wo_0, wo_1 = first_call(n_tp, n_cp, hidden, w_q, w_k, w_v, w_o, *norms[0])
        following = [w_q, w_k, w_v, *norms[1], k_cache, v_cache, wo_1]
        x_1, _, q_1, k_all, vt_all, k_cache, v_cache, wo_1 = block_call(0, n_tp, n_cp, o_0, w_o, wo_0, hidden, w_gate, w_up, w_down, gains[0, 1:], following=following)
        o_1, gathered = global_call(n_tp, q_1, k_all, vt_all, dim)
        x_2, _ = block_call(1, n_tp, n_cp, o_1, w_o, wo_1, x_1, w_gate, w_up, w_down, gains[1, 1:], gathered=gathered)
        return x_2, *[a.reshape(PAIR, rows, n_kv, dim) for a in (k_cache, v_cache)]

    return jax.shard_map(
        device_fn,
        mesh=mesh,
        in_specs=(row_spec, P(('dp', 'cp')), col_spec, col_spec, col_spec, row_w_spec, col_spec, col_spec, row_w_spec, P(), P()),
        out_specs=(row_spec, cache_spec, cache_spec),
        check_vma=False,
    )
```

time: 2030 us -> 782 us (0.39)
  the two profiles are of different devices: /device:TPU:97 before, /device:TPU:103 now
where the time goes in v1:
time: 782 us; the launch traced here: 773 us
  Pallas kernels  748 us (96%)
  local copies, waits for them, and re-layouts  16.8 us (2%)
    pallas_call x2, Pallas kernels, block_call(): pl.pallas_call(functools.partial(block_kernel, layer, n_tp, n_cp, tm, nt,...  555 us
    pallas_call x1, Pallas kernels, first_call(): pl.pallas_call(functools.partial(first_kernel, n_q, n_kv, n_tp, n_cp, 80,...  113 us
    pallas_call x1, Pallas kernels, global_call(): pl.pallas_call(functools.partial(global_kernel, groups, n_tp, unit), in_s...  80 us

profile of v1, /device:TPU:103, one launch (start us, length us, event | category | flops | bytes accessed | tf_op | source)
XLA Modules:
  0.0 773.1 jit_solution(13996538625428001608)
XLA Ops:
  0.6 0.7 convert_element_type.4
  1.3 0.7 broadcast_add_fusion.1
  2.0 0.6 slice_bitcast_fusion.4
  2.6 0.9 broadcast_add_fusion
  3.6 0.6 slice_bitcast_fusion.2
  4.2 0.7 slice_bitcast_fusion
  4.9 5.3 multiply_sine_fusion
  10.2 112.6 %first.1 = (bf16[1024,1024]{1,0:T(8,128)(2,1)}, bf16[2,1024,512]{2,1,0:T(8,128)(2,1)}, bf16[2,1024,512]{2,1,0:T(8,128)(2,1)}, bf16[4,1024,3840]{2,1,0:T(8,128)(2,1)}, bf16[4,1024,3840]{2,1,0:T(8,128)(2,1)}) custom-call(bf16[1024,3840]{1,0:T(8,128)(2,1)} %refs_3_.1, bf16[2,3840,512]{2,1,0:T(8,128)(2,1)} %refs_9_.1, bf16[2,3840,512]{2,1,0:T(8,128)(2,1)} %refs_10_.1, ...), custom_call_target="tpu_custom_call" | custom-call | flops 16106127360 | bytes 15728640 | tf_op jit(solution)/shard_map/first/pallas_call | solution.py:283
  122.8 311.4 %block_0.1 = (bf16[1024,3840]{1,0:T(8,128)(2,1)}, bf16[3,1024,1024]{2,1,0:T(8,128)(2,1)}, bf16[1024,1024]{1,0:T(8,128)(2,1)}, bf16[8192,512]{1,0:T(8,128)(2,1)},...) custom-call(bf16[1024,1024]{1,0:T(8,128)(2,1)} %get-tuple-element.18, ...), custom_call_target="tpu_custom_call", output_to_operand_aliasing={{7}: (18, {}), {6}: (17, {}), {5}: (16, {})} | custom-call | flops 245618442240 | bytes 479723520 | tf_op jit(solution)/shard_map/block_0/pallas_call | solution.py:975
  434.2 80.0 %attend_global.1 = (bf16[1024,1024]{1,0:T(8,128)(2,1)}, bf16[3,1024,1024]{2,1,0:T(8,128)(2,1)}) custom-call(bf16[1024,1024]{1,0:T(8,128)(2,1)} %get-tuple-element.23.q_ref, bf16[8192,512]{1,0:T(8,128)(2,1)} %get-tuple-element.24.k_hbm, bf16[512,8192]{1,0:T(8,128)(2,1)} %get-tuple-element.25.vt_hbm), custom_call_target="tpu_custom_call" | custom-call | flops 17179869184 | bytes 16777216 | tf_op jit(solution)/shard_map/attend_global/pallas_call | solution.py:476
  514.2 243.9 %block_1.1 = (bf16[1024,3840]{1,0:T(8,128)(2,1)}, bf16[3,1024,1024]{2,1,0:T(8,128)(2,1)}) custom-call(bf16[1024,1024]{1,0:T(8,128)(2,1)} %get-tuple-element.26.refs_0_, bf16[2,1024,3840]{2,1,0:T(8,128)(2,1)} %refs_1_.3, bf16[4,1024,3840]{2,1,0:T(8,128)(2,1)} %get-tuple-element.27.refs_2_, ...), custom_call_target="tpu_custom_call", output_to_operand_aliasing={{1}: (8, {})} | custom-call | flops 245618442240 | bytes 479723520 | tf_op jit(solution)/shard_map/block_1/pallas_call | solution.py:975
  758.1 4.0 reshape.23
  762.0 4.0 reshape.24
  766.0 7.0 copy.23
  (1 shorter events, 0.0 us)

commit v2 on v1

--- a/solution.py
+++ b/solution.py
@@ -1,4 +1,5 @@
 import functools
+import types
 import jax
 import jax.numpy as jnp
 from jax import lax
@@ -23,6 +24,7 @@
 BIG_VMEM = 67_000_000
 DMA = pltpu.SemaphoreType.DMA
 VM = pltpu.VMEM
+GATHER_SEMS = [DMA((3, PAIR))] * 8 + [DMA((6, 3))] * PAIR
 
 
 def span(start, size, unit=16):
@@ -62,6 +64,10 @@
     pl.semaphore_wait(barrier, len(peers))
 
 
+def gain_of(ref, layer, row):
+    return 1.0 + ref[layer, row:row + 1, :]
+
+
 def around(axis, n, *distances):
     return [lax.rem(lax.axis_index(axis) + n + d, n) for d in distances]
 
@@ -94,116 +100,132 @@
     return jnp.concatenate([lower * cosine - upper * sine, upper * cosine + lower * sine], axis=-1).astype(BF)
 
 
+def weight_gather(n_tp, n_cp, strip, cut, shard, whole, y1s, y1r, y2s, y2r, x1s=None, x1r=None, x2s=None, x2r=None, rs=None, rr=None):
+    n_x = n_cp // PAIR
+    half = whole.shape[1] // PAIR
+    shared = (half - n_x * strip) // PAIR
+    me, cp = lax.axis_index('tp'), lax.axis_index('cp')
+    chip, base = cp // PAIR, lax.rem(cp, PAIR) * half
+    right, left, opposite = tp_peers(n_tp)
+    sides, sources = on('tp', right, left), (left, right, opposite)
+    *ends, _, partner = on('cp', *cp_peers(n_cp))
+
+    def strip_of(distance):
+        return base + PAIR * shared + lax.rem(chip + n_x + distance, n_x) * strip
+
+    pieces = ((strip_of(0), strip, strip // PAIR), (base, shared, shared // PAIR), (base + shared, shared, shared // PAIR))
+    count = len(pieces)
+
+    def halves(first, size, cut):
+        return span(first, cut), span(first + cut, size - cut)
+
+    def y_first(p):
+        at = span(*pieces[p][:PAIR])
+        return [send(shard.at[at, :], whole.at[me, at, :], y1s.at[p, d], y1r.at[p, d], sides[d]) for d in TWO]
+
+    def y_second(p):
+        refs = [whole.at[sources[d], halves(*pieces[p])[d], :] for d in TWO]
+        return [send(refs[d], refs[d], y2s.at[p, d], y2r.at[p, d], sides[d]) for d in TWO]
+
+    def x_first(s):
+        ref = whole.at[sources[s], span(strip_of(0), strip), :]
+        return [send(ref, ref, x1s.at[s, d], x1r.at[s, d], ends[d]) for d in TWO]
+
+    def x_second(s):
+        refs = [whole.at[sources[s], halves(strip_of((-1, 1)[d]), strip, cut)[d], :] for d in TWO]
+        return [send(refs[d], refs[d], x2s.at[s, d], x2r.at[s, d], ends[d]) for d in TWO]
+
+    def relay(kind, s):
+        first, size = pieces[kind][:PAIR] if kind < count else (strip_of(kind + 1 - count), strip)
+        ref = whole.at[sources[s], span(first, size), :]
+        return [send(ref, ref, rs.at[kind, s], rr.at[kind, s], partner)]
+
+    def y_stage(p, *more):
+        arrived(y_first(p))
+        start(y_second(p), *more, *[relay(p, s) for s in TWO])
+
+    def y_end(p):
+        arrived(y_second(p))
+        start(relay(p, PAIR))
+
+    def x_stage(s):
+        arrived(x_first(s))
+        start(x_second(s), relay(count, s), relay(count + PAIR, s))
+
+    def x_end(s):
+        arrived(x_second(s))
+        start(relay(count + 1, s))
+
+    def drain(parts):
+        for s in TRIO:
+            wait(*[relay(kind, s) for kind in range(PAIR * count)])
+            departed(x_first(s), x_second(s))
+        for p in parts:
+            departed(y_first(p), y_second(p))
+
+    peers = (*sides, *ends, partner)
+    return types.SimpleNamespace(**{f.__name__: f for f in (y_first, y_second, x_first, x_second, relay, y_stage, y_end, x_stage, x_end, drain)}, peers=peers)
+
+
+def keep_heads(rows_ref, out_ref):
+    dim = out_ref.shape[-1]
+
+    @pl.loop(0, out_ref.shape[1] // LANES)
+    def _(i):
+        at = span(i * LANES, LANES)
+        for t in TWO:
+            out_ref[t, at] = jnp.stack([rows_ref[t, at, begin:begin + dim] for begin in range(0, rows_ref.shape[-1], dim)], axis=1)
+
+
 def first_kernel(
     n_q, n_kv, n_tp, n_cp, strip, cut,
-    x_ref, wk_ref, wv_ref, wq_ref, gain_ref, qg_ref, kg_ref, cos_ref, sin_ref, wo_hbm,
-    o_hbm, kc_hbm, vc_hbm, wo_all, wo_next,
-    h_ref, q_ref, kv_ref, past_ref,
-    y1s, y1r, y2s, y2r, x1s, x1r, x2s, x2r, rs, rr, ks, kr, csem, osem,
+    x_ref, wk_ref, wv_ref, wq_ref, gain_ref, hg_ref, cos_ref, sin_ref, wo_hbm,
+    o_hbm, kc_hbm, vc_hbm, wo_all,
+    h_ref, q_ref, kv_ref, past_ref, cache_ref,
+    ks, kr, csem, osem, *sems,
 ):
     step = pl.program_id(0)
     rows = x_ref.shape[0]
-    dim = qg_ref.shape[-1]
-    o_rows = wo_hbm.shape[1]
-    n_x = n_cp // PAIR
-    shared = (o_rows // PAIR - n_x * strip) // PAIR
-
-    me, cp = lax.axis_index('tp'), lax.axis_index('cp')
-    core, chip = lax.rem(cp, PAIR), cp // PAIR
-    right, left, opposite = tp_peers(n_tp)
-    sides, sources = on('tp', right, left), (left, right, opposite)
-    *ends, _, partner = on('cp', *cp_peers(n_cp))
+    dim = hg_ref.shape[-1]
+    g = weight_gather(n_tp, n_cp, strip, cut, wo_hbm.at[0], wo_all, *sems)
     follow, prior = on('cp', *around('cp', n_cp, 1, -1))
-    base = core * (o_rows // PAIR)
-
-    def strip_of(distance):
-        return base + PAIR * shared + lax.rem(chip + n_x + distance, n_x) * strip
-
-    piece = o_rows // n_cp
-    pieces = ((strip_of(0), strip, cut), (base, shared, shared // PAIR), (base + shared, shared, shared // PAIR), (cp * piece, piece, piece // PAIR))
-    final = len(pieces) - 1
-
-    def target(p):
-        return wo_next if p == final else wo_all
-
-    def y_first(p):
-        at = span(*pieces[p][:PAIR])
-        return [send(wo_hbm.at[p // final, at, :], target(p).at[me, at, :], y1s.at[p, d], y1r.at[p, d], sides[d]) for d in TWO]
-
-    def halves(first, size, cut):
-        return span(first, cut), span(first + cut, size - cut)
-
-    def y_second(p):
-        refs = [target(p).at[sources[d], halves(*pieces[p])[d], :] for d in TWO]
-        return [send(refs[d], refs[d], y2s.at[p, d], y2r.at[p, d], sides[d]) for d in TWO]
-
-    def x_first(s):
-        ref = wo_all.at[sources[s], span(strip_of(0), strip), :]
-        return [send(ref, ref, x1s.at[s, d], x1r.at[s, d], ends[d]) for d in TWO]
-
-    def x_second(s):
-        refs = [wo_all.at[sources[s], halves(strip_of((-1, 1)[d]), strip, cut)[d], :] for d in TWO]
-        return [send(refs[d], refs[d], x2s.at[s, d], x2r.at[s, d], ends[d]) for d in TWO]
-
-    def relay(kind, s):
-        first, size = pieces[kind][:PAIR] if kind < final else (strip_of(kind - PAIR), strip)
-        ref = wo_all.at[sources[s], span(first, size), :]
-        return [send(ref, ref, rs.at[kind, s], rr.at[kind, s], partner)]
 
     def send_kv(t):
         return [send(kv_ref.at[t], past_ref.at[t], ks.at[t], kr.at[t], follow)]
 
     def keep_kv(t):
-        return [pltpu.make_async_copy(kv_ref.at[t], (kc_hbm, vc_hbm)[t].at[0], csem.at[t])]
+        return [pltpu.make_async_copy(cache_ref.at[t], (kc_hbm, vc_hbm)[t].at[0], csem.at[t])]
 
     group = n_q // n_kv
 
-    def keep_o(h):
-        some = pl.ds(h * group * dim, group * dim)
-        return [pltpu.make_async_copy(q_ref.at[:, some], o_hbm.at[:, some], osem.at[h])]
-
-    def y_stage(p, *more):
-        arrived(y_first(p))
-        start(y_second(p), *more, *[relay(p, s) for s in TWO if p < final])
-
-    def x_stage(s):
-        arrived(x_first(s))
-        start(x_second(s), relay(final, s), relay(final + PAIR, s))
-
-    def y_end(p):
-        arrived(y_second(p))
-        start(relay(p, PAIR), *([] if p else [x_first(PAIR)]))
-
-    def x_end(s):
-        arrived(x_second(s))
-        start(relay(final + 1, s))
+    keep_o = [pltpu.make_async_copy(q_ref, o_hbm, osem)]
 
     q_step = PAIR * n_kv
 
     @pl.when(step == 0)
     def _():
-        greet((*sides, *ends, follow, prior))
-        start(*map(y_first, TWO))
+        greet((*g.peers[:-1], follow, prior))
+        start(*map(g.y_first, TWO))
         rb = 32
 
         @pl.loop(0, rows // rb)
         def _(i):
             at = span(i * rb, rb)
             xf = x_ref[at, :].astype(F32)
-            h_ref[at, :] = (xf * mean_scale(xf) * gain_ref[...]).astype(BF)
+            h_ref[at, :] = (xf * mean_scale(xf) * gain_of(gain_ref, 0, 0)).astype(BF)
 
     @pl.when(step == n_kv)
     def _():
-        start(send_kv(0), keep_kv(0))
+        start(send_kv(0))
 
     @pl.when(step == q_step)
     def _():
-        start(send_kv(1), keep_kv(1))
-        y_stage(0, y_first(PAIR), *map(x_first, TWO))
+        g.y_stage(0, g.y_first(PAIR), *map(g.x_first, TWO))
+        start(send_kv(1))
 
     @pl.when(step == q_step + 3)
     def _():
-        x_stage(0)
+        g.x_stage(0)
 
     def project(w_ref, store, finish):
         @pl.loop(0, rows // TILE)
@@ -219,12 +241,12 @@
     def into_q(at, value):
         q_ref[at, span((step - q_step) * dim, dim, LANES)] = value
 
-    def rotate(gain_ref):
-        return lambda a, at: rotate_heads(a, gain_ref[...], cos_ref[at, :], sin_ref[at, :])
+    def rotate(row):
+        return lambda a, at: rotate_heads(a, gain_of(hg_ref, 0, row), cos_ref[at, :], sin_ref[at, :])
 
     @pl.when(step < n_kv)
     def _():
-        project(wk_ref, into_kv(0, step), rotate(kg_ref))
+        project(wk_ref, into_kv(0, step), rotate(1))
 
     @pl.when((step >= n_kv) & (step < q_step))
     def _():
@@ -232,66 +254,68 @@
 
     @pl.when(step >= q_step)
     def _():
-        project(wq_ref, into_q, rotate(qg_ref))
-
-    def attend(h):
-        head = slice(h * dim, (h + 1) * dim)
-        for g in range(group):
-            local_head(q_ref, h * group + g, *[ref.at[t, :, head] for t in TWO for ref in (past_ref, kv_ref)])
-        start(keep_o(h))
+        project(wq_ref, into_q, rotate(0))
 
     @pl.when(step == q_step + n_q - 1)
     def _():
-        y_stage(1, y_first(final))
-        y_end(0)
-        x_stage(1)
+        keep_heads(kv_ref, cache_ref)
+        start(*map(keep_kv, TWO))
+        g.y_stage(1)
+        g.y_end(0)
+        start(g.x_first(PAIR))
+        g.x_stage(1)
+        g.y_stage(PAIR)
         arrived(*map(send_kv, TWO))
-        attend(0)
-        x_end(0)
-        y_stage(PAIR)
-        x_stage(PAIR)
-        y_stage(final)
-        for h in range(1, n_kv):
-            attend(h)
-        x_end(1)
-        y_end(1)
-        y_end(PAIR)
-        x_end(PAIR)
-        arrived(y_second(final))
+
+        @pl.loop(0, n_kv)
+        def _(h):
+            head = span(h * dim, dim, LANES)
+
+            @pl.loop(0, group)
+            def _(i):
+                local_head(q_ref, h * group + i, *[ref.at[t, :, head] for t in TWO for ref in (past_ref, kv_ref)])
+
+            @pl.when(h == 0)
+            def _():
+                g.x_end(0)
+                g.x_stage(PAIR)
+
+        start(keep_o)
+        g.x_end(1)
+        g.y_end(1)
+        g.y_end(PAIR)
+        g.x_end(PAIR)
         departed(*map(send_kv, TWO))
-        wait(*map(keep_kv, TWO), *map(keep_o, range(n_kv)))
-        for s in TRIO:
-            wait(*[relay(kind, s) for kind in range(PAIR * len(TRIO))])
-            departed(x_first(s), x_second(s))
-        for p in range(len(pieces)):
-            departed(y_first(p), y_second(p))
-
-
-def first_call(n_tp, n_cp, x, w_q, w_k, w_v, w_o, gain, q_gain, k_gain, cosine, sine):
+        wait(*map(keep_kv, TWO), keep_o)
+        g.drain(TRIO)
+
+
+def first_call(n_tp, n_cp, x, w_q, w_k, w_v, w_o, gain, head_gain, cosine, sine):
     rows, width = x.shape
-    dim = q_gain.shape[-1]
+    dim = head_gain.shape[-1]
     n_q, n_kv = w_q.shape[-1] // dim, w_k.shape[-1] // dim
     at_k = lambda t: jnp.minimum(t, n_kv - 1)
     at_v = lambda t: jnp.clip(t - n_kv, 0, n_kv - 1)
     at_q = lambda t: jnp.maximum(t - PAIR * n_kv, 0)
-    whole = lambda a: pl.BlockSpec(a.shape, lambda t: TWO[:1] * PAIR, pipeline_mode=pl.Buffered(1))
+    whole = lambda a: pl.BlockSpec(a.shape, lambda t: TWO[:1] * a.ndim, pipeline_mode=pl.Buffered(1))
     w_spec = lambda at: pl.BlockSpec((1, width, dim), lambda t: (0, 0, at(t)))
     shape = lambda *sizes: jax.ShapeDtypeStruct(sizes, BF)
     q_width, kv_width = n_q * dim, n_kv * dim
     work = PAIR * width * (q_width + PAIR * kv_width)
-    gathered, cache = shape(n_tp, *w_o.shape[1:]), shape(PAIR, rows, kv_width)
+    gathered, cache = shape(n_tp, *w_o.shape[1:]), shape(PAIR, rows, n_kv, dim)
+    flat = (PAIR, rows, kv_width)
     return pl.pallas_call(
-        functools.partial(first_kernel, n_q, n_kv, n_tp, n_cp, 80, 48),
+        functools.partial(first_kernel, n_q, n_kv, n_tp, n_cp, 64, 16),
         grid=(n_q + PAIR * n_kv,),
-        in_specs=[whole(x), *map(w_spec, (at_k, at_v, at_q)), *map(whole, (gain, q_gain, k_gain, cosine, sine)), ANY],
-        out_specs=[ANY] * 5,
-        out_shape=[shape(rows, q_width), cache, cache, gathered, gathered],
-        scratch_shapes=[VM((rows, width), BF), VM((rows, q_width), BF), VM(cache.shape, BF), VM(cache.shape, BF)]
-        + [DMA((4, PAIR))] * 8 + [DMA((6, 3))] * PAIR + [DMA((PAIR,))] * 3 + [DMA((n_kv,))],
+        in_specs=[whole(x), *map(w_spec, (at_k, at_v, at_q)), *map(whole, (gain, head_gain, cosine, sine)), ANY],
+        out_specs=[ANY] * 4,
+        out_shape=[shape(rows, q_width), cache, cache, gathered],
+        scratch_shapes=[VM((rows, width), BF), VM((rows, q_width), BF), VM(flat, BF), VM(flat, BF), VM(cache.shape, BF)]
+        + [DMA((PAIR,))] * 3 + [DMA] + GATHER_SEMS,
         compiler_params=pltpu.CompilerParams(dimension_semantics=("arbitrary",), collective_id=2, has_side_effects=True, vmem_limit_bytes=BIG_VMEM),
         cost_estimate=pl.CostEstimate(flops=rows * work, bytes_accessed=work, transcendentals=0),
         name="first",
-    )(x, w_k, w_v, w_q, gain, q_gain, k_gain, cosine, sine, w_o)
+    )(x, w_k, w_v, w_q, gain, head_gain, cosine, sine, w_o)
 
 
 def scores_of(q, k):
@@ -307,7 +331,7 @@
     col = lax.broadcasted_iota(jnp.int32, (tile, tile), 1)
     for begin in range(0, rows, tile):
         end = begin + tile
-        at = (slice(begin, end), slice(head * dim, (head + 1) * dim))
+        at = (slice(begin, end), span(head * dim, dim, LANES))
         q = q_ref[at]
         past = scores_of(q, kp_ref[begin:, :])
         here = scores_of(q, ko_ref[:end, :])
@@ -343,9 +367,9 @@
 
 
 def global_kernel(
-    groups, n_tp, unit, q_ref, k_hbm, vt_hbm, o_hbm, og_hbm,
+    groups, n_tp, n_cp, unit, strip, cut, q_ref, k_hbm, vt_hbm, wo_hbm, _, o_hbm, og_hbm, wn_hbm,
     k_ref, vt_ref, o_ref, m_ref, l_ref, ka_ref, kb_ref, xa_ref, xb_ref, acc_ref, sa_ref, sb_ref, pa_ref, pb_ref,
-    ksem, vsem, osem, s1, r1, s2, r2,
+    ksem, vsem, osem, s1, r1, s2, r2, *sems,
 ):
     rows, width = q_ref.shape
     dim = acc_ref.shape[0]
@@ -356,7 +380,8 @@
     cp = lax.axis_index('cp')
     base = cp * (rows // block)
     last = base - 1
-    sides, first, second = row_gather(n_tp, unit, og_hbm, o_ref, s1, r1, s2, r2)
+    _, first, second = row_gather(n_tp, unit, og_hbm, o_ref, s1, r1, s2, r2)
+    w = weight_gather(n_tp, n_cp, strip, cut, wo_hbm.at[1], wn_hbm, *sems)
     ready = tile // unit
 
     def load(b):
@@ -367,11 +392,14 @@
         at = span(i * tile, tile)
         return [pltpu.make_async_copy(o_ref.at[at, :], o_hbm.at[at, :], osem.at[i])]
 
-    @pl.loop(0, cp + 1)
+    start(load(cp))
+
+    @pl.loop(0, cp)
     def _(b):
-        start(load(cp - b))
-
-    greet(sides)
+        start(load(b))
+
+    greet(w.peers)
+    start(w.y_first(1), w.y_first(PAIR), *map(w.x_first, TRIO), *[w.relay(0, s) for s in TRIO])
     wait(load(cp))
 
     key = lax.broadcasted_iota(jnp.int32, (block, wide), 0)
@@ -381,12 +409,6 @@
     def _(turn):
         i, h = turn // n_kv, lax.rem(turn, n_kv)
         head = span(h * dim, dim, LANES)
-
-        @pl.when(turn == 0)
-        def _():
-            @pl.loop(0, cp)
-            def _(b):
-                wait(load(b))
 
         q = jnp.concatenate([q_ref[span(i * tile, tile), span((h * groups + g) * dim, dim, LANES)] for g in range(groups)], axis=0)
 
@@ -423,8 +445,14 @@
             soften(sa_ref, xa_ref, pa_ref, ka_ref)
             weigh(base + b, pa_ref, ka_ref)
 
+        def loaded(b):
+            @pl.when((turn == 0) & (b < cp))
+            def _():
+                wait(load(b))
+
         @pl.when(cp > 0)
         def _():
+            loaded(0)
             score(jnp.int32(0), sa_ref, xa_ref)
             pb_ref[...] = jnp.zeros_like(pb_ref)
             kb_ref[...] = jnp.ones_like(kb_ref)
@@ -432,6 +460,7 @@
             @pl.loop(0, base // PAIR)
             def _(half):
                 b = PAIR * half
+                loaded(half + 1)
                 score(b + 1, sb_ref, xb_ref)
                 soften(sa_ref, xa_ref, pa_ref, ka_ref)
                 weigh(jnp.maximum(b - 1, 0), pb_ref, kb_ref)
@@ -445,12 +474,21 @@
         for g in range(groups):
             o_ref[span(i * tile, tile), span((h * groups + g) * dim, dim, LANES)] = out[g * tile:(g + 1) * tile]
 
+        @pl.when(turn == 0)
+        def _():
+            w.y_stage(1)
+            w.x_stage(0)
+
         @pl.when(turn == n_kv - 1)
         def _():
             start(store(0), *map(first, range(ready)))
+            w.y_stage(PAIR)
+            w.x_stage(1)
 
         @pl.when(turn == n_kv)
         def _():
+            w.x_stage(PAIR)
+            w.y_end(1)
             for u in range(ready - 1):
                 arrived(first(u))
                 start(second(u))
@@ -458,13 +496,18 @@
     start(store(1))
     arrived(first(ready - 1))
     start(second(ready - 1))
+    w.x_end(0)
+    w.x_end(1)
+    w.y_end(PAIR)
+    w.x_end(PAIR)
     for u in range(ready):
         departed(first(u))
         wait(second(u))
     wait(*map(store, TWO))
-
-
-def global_call(n_tp, q, k_all, vt_all, dim):
+    w.drain(TRIO[1:])
+
+
+def global_call(n_tp, n_cp, strip, cut, q, k_all, vt_all, w_o, wo_next, dim):
     rows, width = q.shape
     every, kv_width = k_all.shape
     groups = width // kv_width
@@ -474,19 +517,20 @@
     vmem = pl.BlockSpec(memory_space=VM)
     row, slab = VM((1, wide), F32), VM((8, wide), F32)
     return pl.pallas_call(
-        functools.partial(global_kernel, groups, n_tp, unit),
-        in_specs=[vmem, ANY, ANY],
-        out_specs=[ANY, ANY],
-        out_shape=[jax.ShapeDtypeStruct(q.shape, BF), jax.ShapeDtypeStruct((n_tp - 1, *q.shape), BF)],
+        functools.partial(global_kernel, groups, n_tp, n_cp, unit, strip, cut),
+        in_specs=[vmem] + [ANY] * 4,
+        out_specs=[ANY] * 3,
+        out_shape=[jax.ShapeDtypeStruct(size, BF) for size in (q.shape, (n_tp - 1, *q.shape), wo_next.shape)],
+        input_output_aliases={4: PAIR},
         scratch_shapes=[VM(k_all.shape, BF), VM(vt_all.shape, BF), VM(q.shape, BF), row, slab, row, row, slab, slab, VM((dim, wide), F32)]
-        + [VM((tile, wide), t) for t in (F32, F32, BF, BF)] + [DMA((every // rows,))] * PAIR + [DMA((PAIR,))] + [DMA((tile // unit, PAIR))] * 4,
+        + [VM((tile, wide), t) for t in (F32, F32, BF, BF)] + [DMA((every // rows,))] * PAIR + [DMA((PAIR,))] + [DMA((tile // unit, PAIR))] * 4 + GATHER_SEMS,
         compiler_params=pltpu.CompilerParams(collective_id=3, has_side_effects=True, vmem_limit_bytes=BIG_VMEM),
         cost_estimate=pl.CostEstimate(flops=PAIR * rows * every * width, bytes_accessed=PAIR * every * width, transcendentals=0),
         name="attend_global",
-    )(q, k_all, vt_all)
-
-
-def block_kernel(layer, n_tp, n_cp, tm, nt, unit, ready, follow, *refs):
+    )(q, k_all, vt_all, w_o, wo_next)
+
+
+def block_kernel(layer, n_tp, n_cp, tm, nt, unit, strip, cut, ready, follow, *refs):
     queue = iter(refs)
 
     def take(names):
@@ -496,14 +540,15 @@
     if ready:
         take(1)
     if follow:
-        wq_hbm, wk_hbm, wv_hbm, hg_ref, qg_ref, kg_ref, cos_ref, sin_ref, *_ = take(11)
+        wq_hbm, wk_hbm, wv_hbm, hg_ref, cos_ref, sin_ref, *_ = take(8)
     out_hbm, og_hbm = take(PAIR)
     if follow:
         q_hbm, ka_hbm, va_hbm, k_hbm, v_hbm, wn_hbm = take(6)
-    wbuf, pbuf, r1, r2, xb, mbuf, sbuf, obuf, xbuf, rown, wsem, osem, xsem, stsem = take(14)
+    wbuf, pbuf, r1, r2, xb, mbuf, sbuf, gbuf, obuf, xbuf, rown, wsem, osem, xsem, stsem = take(15)
     o1s, o1r, o2s, o2r, s1s, s1r, sbs, sbr, sas, sar, g1s, g1r, g2s, g2r = take(14)
     if follow:
-        nbuf, vbuf, nsem, fs, fr, hs, hr, ps, pr, a1s, a1r, a2s, a2r, bs, br_ = take(15)
+        nbuf, vbuf, cbuf, nsem, fs, fr, hs, hr, ps, pr, *sems = take(14)
+        w = weight_gather(n_tp, n_cp, strip, cut, wo_own.at[layer + 1], wn_hbm, *sems)
 
     rows, width = x_hbm.shape
     o_width = o_hbm.shape[1]
@@ -519,7 +564,7 @@
     depth, lag = 3, PAIR
     n_n = 0
     if follow:
-        dim = qg_ref.shape[-1]
+        dim = hg_ref.shape[-1]
         nw = wk_hbm.shape[-1]
         n_qt = wq_hbm.shape[-1] // nw
         n_n = n_qt + PAIR
@@ -654,7 +699,7 @@
             at = pl.ds(begin, sub)
             z = sum([r2[k, d, at, :] for d in TWO], p[span(lax.rem(k, fine) * unit + me * br + begin, sub), :])
             r = rown[lax.rem(k // fine, PAIR), lax.rem(k, fine), at, :].astype(F32)
-            xb[k, at, :] = (r + z * mean_scale(z) * gain_ref[PAIR:, :]).astype(BF)
+            xb[k, at, :] = (r + z * mean_scale(z) * gain_of(gain_ref, layer, 3)).astype(BF)
         start(x_first(k), x_own(k))
         for d in TWO:
             departed(s_far(k, d), s_plain(k, d), s_sum(k, d))
@@ -698,7 +743,7 @@
     def stores(c):
         k, first, size = c
         at, slot, some = span(first, size), lax.rem(k, depth), head_of(size)
-        pairs = [(kv_mine(c, t), kv_at(c, cp, t)) for t in TWO] + [(nbuf.at[slot, t, some, :], (k_hbm, v_hbm)[t].at[1, at, :]) for t in TWO]
+        pairs = [(kv_mine(c, t), kv_at(c, cp, t)) for t in TWO] + [(cbuf.at[slot, t, some], (k_hbm, v_hbm)[t].at[1, at]) for t in TWO]
         pairs += [(nbuf.at[slot, PAIR + t, some, :], q_hbm.at[at, pl.ds(t * nw, nw)]) for t in range(n_qt)]
         return [pltpu.make_async_copy(src, dst, nsem.at[slot, t]) for t, (src, dst) in enumerate(pairs)]
 
@@ -714,22 +759,38 @@
         def _(i):
             rows_of = span(i * sub, sub)
             xf = xbuf[rows_of, :].astype(F32)
-            mbuf[rows_of, :] = (xf * mean_scale(xf) * hg_ref[...]).astype(BF)
+            mbuf[rows_of, :] = (xf * mean_scale(xf) * gain_of(gain_ref, layer + 1, 0)).astype(BF)
 
         cosine, sine = cos_ref[at, :], sin_ref[at, :]
-        for t in range(n_n):
+
+        def project(t, finish):
             start_w(base + t + PAIR)
             w_slot = lax.rem(base + t, depth)
             pltpu.make_async_copy(wk_hbm.at[layer + 1], narrow(w_slot), wsem.at[w_slot, 0]).wait()
-            acc = jnp.dot(mbuf[some, :], narrow(w_slot)[...], preferred_element_type=F32)
-            if t == 1:
-                nbuf[slot, t, some, :] = acc.astype(BF)
-                vbuf[slot, :, some] = acc.T.astype(BF)
-                start(kv_first(c))
-            else:
-                for begin in range(0, nw, dim):
-                    this = slice(begin, begin + dim)
-                    nbuf[slot, t, some, this] = rotate_heads(acc[:, this], qg_ref[...] if t else kg_ref[...], cosine, sine)
+
+            @pl.loop(0, nw // dim)
+            def _(h):
+                this = span(h * dim, dim, LANES)
+                finish(this, jnp.dot(mbuf[some, :], wbuf[w_slot, head_of(width), this], preferred_element_type=F32))
+
+        def rotate(t, row):
+            def finish(this, acc):
+                nbuf[slot, t, some, this] = rotate_heads(acc, gain_of(hg_ref, layer + 1, row), cosine, sine)
+            return finish
+
+        def plain(this, acc):
+            nbuf[slot, 1, some, this] = acc.astype(BF)
+            vbuf[slot, this, some] = acc.T.astype(BF)
+
+        project(0, rotate(0, 1))
+        project(1, plain)
+        start(kv_first(c))
+
+        @pl.loop(PAIR, n_n)
+        def _(t):
+            project(t, rotate(t, 0))
+
+        keep_heads(nbuf.at[slot, :, some], cbuf.at[slot, :, some])
         start(stores(c))
 
     def f1(c):
@@ -746,42 +807,10 @@
         wait(*[kv_relay(c, e) for e in TRIO])
         departed(kv_second(c))
 
-    piece = o_width // n_cp
-
-    def strips(s, dev, size=piece, part=0):
-        return wn_hbm.at[lax.rem(me + 1 + s, n_tp), span(dev * piece + part * size, size), :]
-
-    def a_first(s):
-        ref = strips(s, cp)
-        return [send(ref, ref, a1s.at[s, d], a1r.at[s, d], ends[d]) for d in TWO]
-
-    def a_second(s):
-        refs = [strips(s, (behind, ahead)[d], piece // PAIR, d) for d in TWO]
-        return [send(refs[d], refs[d], a2s.at[s, d], a2r.at[s, d], ends[d]) for d in TWO]
-
-    def a_relay(s, *kinds):
-        refs = {e: strips(s, (cp, behind, ahead, across)[e]) for e in kinds}
-        return [send(ref, ref, bs.at[s, e], br_.at[s, e], partner) for e, ref in refs.items()]
-
-    def a_serve(s):
-        arrived(a_first(s))
-        start(a_second(s), a_relay(s, *TRIO[1:]))
-
-    def a_finish(s):
-        arrived(a_second(s))
-        start(a_relay(s, len(TRIO)))
-
-    def a_drain(s):
-        wait(a_relay(s, *TRIO, len(TRIO)))
-        departed(a_first(s), a_second(s))
-
     for t in TWO:
         start_w(jnp.int32(t))
     greet((*sides, *ends, partner) if follow else sides)
     start(*[o_first(ready + t) for t in TWO])
-    if follow:
-        for s in TRIO:
-            start(a_first(s), a_relay(s, 0))
     served = ready
     if not ready:
         for served in TWO:
@@ -802,6 +831,23 @@
             copies.append(pltpu.make_async_copy(src.at[at, :], obuf.at[:, pl.ds(s * o_width, o_width)], osem.at[s]))
         return copies
 
+    def between(n, j):
+        @pl.when((j == 0) & (n >= 1))
+        def _():
+            all_of(e1, n - 1)
+
+        @pl.when(j == 1)
+        def _():
+            serve(n, PAIR)
+
+            @pl.when(n >= lag)
+            def _():
+                all_of(e3, n - lag)
+
+        @pl.when(j == depth)
+        def _():
+            serve(n, depth)
+
     def chunk(n, _):
         base = base_of(n)
         slot_p = lax.rem(n, PAIR)
@@ -837,42 +883,25 @@
         def _(i):
             at = span(i * sub, sub)
             z = p[at, :]
-            r = (xbuf[at, :].astype(F32) + z * mean_scale(z) * gain_ref[0:1, :]).astype(BF)
+            r = (xbuf[at, :].astype(F32) + z * mean_scale(z) * gain_of(gain_ref, layer, 1)).astype(BF)
             xbuf[at, :] = r
             rf = r.astype(F32)
-            mbuf[at, :] = (rf * mean_scale(rf) * gain_ref[1:2, :]).astype(BF)
+            mbuf[at, :] = (rf * mean_scale(rf) * gain_of(gain_ref, layer, PAIR)).astype(BF)
 
         for i in range(fine):
             rown[slot_p, i] = xbuf[span(i * unit + me * br, br), :]
 
-        @pl.loop(0, n_g)
-        def _(j):
-            index = base + n_o + PAIR * j
+        @pl.loop(0, PAIR * n_g)
+        def _(t):
+            index, j, odd = base + n_o + t, t // PAIR, lax.rem(t, PAIR)
             start_w(index + PAIR)
             slot = wait_w(index, width)
-            gate = jnp.dot(mbuf[...], part_of(slot, width)[...], preferred_element_type=F32)
-            start_w(index + depth)
-            slot = wait_w(index + 1, width)
-            up = jnp.dot(mbuf[...], part_of(slot, width)[...], preferred_element_type=F32)
-            sbuf[:, columns(j)] = (jax.nn.gelu(gate, approximate=True) * up).astype(BF)
-
-            @pl.when((j == 0) & (n >= 1))
+            gbuf[odd] = jnp.dot(mbuf[...], part_of(slot, width)[...], preferred_element_type=F32)
+
+            @pl.when(odd == 1)
             def _():
-                all_of(e1, n - 1)
-                if follow:
-                    a_serve(n - 1)
-
-            @pl.when(j == 1)
-            def _():
-                serve(n, PAIR)
-
-                @pl.when(n >= lag)
-                def _():
-                    all_of(e3, n - lag)
-
-            @pl.when(j == depth)
-            def _():
-                serve(n, depth)
+                sbuf[:, columns(j)] = (jax.nn.gelu(gbuf[0], approximate=True) * gbuf[1]).astype(BF)
+                between(n, j)
 
         @pl.when(n >= 1)
         def _():
@@ -921,23 +950,31 @@
         f0(middle, tail)
     all_of(e3, last)
     if follow:
-        each_strip = lambda step: [step(s) for s in TRIO]
-        each_strip(a_finish)
-        for i, c in enumerate(late):
+        start(w.y_first(0))
+
+        @pl.loop(0, fine)
+        def _(i):
             e4(last * fine + i)
-            f0(c, tail + (1 + i) * n_n)
-            (f2 if i else f1)(middle)
+            f0((chunks - 1 + i, rows - tm + i * unit, unit), tail + (1 + i) * n_n)
+            for t, step in enumerate((f1, f2)):
+                @pl.when(i == t)
+                def _():
+                    step(middle)
+
+        arrived(w.y_first(0))
+        start(w.y_second(0))
         for step in (f1, f2):
             for c in late:
                 step(c)
-        each_strip(a_drain)
+        arrived(w.y_second(0))
+        departed(w.y_first(0), w.y_second(0))
         for c in (batch(every[0]), early, middle, *late):
             f3(c)
     else:
         all_of(e4, last)
 
 
-def block_call(layer, n_tp, n_cp, o, w_o, wo_all, x, w_gate, w_up, w_down, gain, gathered=None, following=None):
+def block_call(layer, n_tp, n_cp, strip, cut, o, w_o, wo_all, x, w_gate, w_up, w_down, gain, gathered=None, following=None):
     rows, width = x.shape
     o_width = o.shape[1]
     hidden = w_down.shape[1]
@@ -951,7 +988,7 @@
     out_shape = [shape(rows, width), shape(n_tp - 1, rows, o_width)]
     scratch = [
         VM((3, deep, nt), BF), VM((PAIR, tm, width), F32), VM((units, PAIR, br, width // PAIR), F32), VM((units, PAIR, br, width), F32),
-        VM((units, br, width), BF), VM((tm, width), BF), VM((tm, hidden), BF), VM((tm, n_tp * o_width), BF), VM((tm, width), BF), VM((PAIR, tm // unit, br, width), BF),
+        VM((units, br, width), BF), VM((tm, width), BF), VM((tm, hidden), BF), VM((PAIR, tm, nt), F32), VM((tm, n_tp * o_width), BF), VM((tm, width), BF), VM((PAIR, tm // unit, br, width), BF),
         DMA((3, n_tp)), DMA((n_tp,)), DMA, DMA((units,)),
     ] + [DMA((units, PAIR))] * 14
     aliases = {}
@@ -963,17 +1000,18 @@
         q_width, kv_width = following[0].shape[-1], following[1].shape[-1]
         n_qt = q_width // kv_width
         operands += following
-        in_specs += [ANY] * 3 + [vmem] * 5 + [ANY] * 3
-        kept = following[-3:]
+        in_specs += [ANY] * 3 + [vmem] * 3 + [ANY] * PAIR
+        kept = following[-PAIR:]
         out_shape += [shape(rows, q_width), shape(n_cp * rows, kv_width), shape(kv_width, n_cp * rows)] + [shape(*a.shape) for a in kept]
         aliases.update((len(operands) - i, len(out_shape) - i) for i in range(1, 1 + len(kept)))
-        scratch += [VM((3, n_qt + PAIR, tm, kv_width), BF), VM((3, kv_width, tm), BF), DMA((3, n_qt + 4))]
+        out_shape.append(shape(*wo_all.shape))
+        scratch += [VM((3, n_qt + PAIR, tm, kv_width), BF), VM((3, kv_width, tm), BF), VM((3, PAIR, tm, *kept[0].shape[PAIR:]), BF), DMA((3, n_qt + 4))]
         late = chunks + 1
-        for count, sizes in ((1, (late, PAIR, 3)), (1, (late, PAIR)), (1, (late, 3, PAIR)), (PAIR, (n_tp - 1, PAIR)), (1, (n_tp - 1, 4))):
+        for count, sizes in ((1, (late, PAIR, 3)), (1, (late, PAIR)), (1, (late, 3, PAIR)), (PAIR, (1, PAIR))):
             scratch += [DMA(sizes)] * (PAIR * count)
     weights = width * (n_tp * o_width + 3 * hidden)
     return pl.pallas_call(
-        functools.partial(block_kernel, layer, n_tp, n_cp, tm, nt, unit, 0 if gathered is None else units // PAIR, following is not None),
+        functools.partial(block_kernel, layer, n_tp, n_cp, tm, nt, unit, strip, cut, 0 if gathered is None else units // PAIR, following is not None),
         in_specs=in_specs,
         out_specs=[ANY] * len(out_shape),
         out_shape=out_shape,
@@ -1002,16 +1040,14 @@
         rows, width = hidden.shape
         dim = qk_gain.shape[-1]
         n_kv = w_k.shape[-1] // dim
-        gains = 1.0 + norm_gain
-        head_gains = 1.0 + qk_gain
         angles = [angles_of(positions, dim, theta) for theta in THETAS]
-        norms = [(gains[l, :1], head_gains[l, :1], head_gains[l, 1:], *angles[l]) for l in TWO]
-        o_0, k_cache, v_cache, wo_0, wo_1 = first_call(n_tp, n_cp, hidden, w_q, w_k, w_v, w_o, *norms[0])
-        following = [w_q, w_k, w_v, *norms[1], k_cache, v_cache, wo_1]
-        x_1, _, q_1, k_all, vt_all, k_cache, v_cache, wo_1 = block_call(0, n_tp, n_cp, o_0, w_o, wo_0, hidden, w_gate, w_up, w_down, gains[0, 1:], following=following)
-        o_1, gathered = global_call(n_tp, q_1, k_all, vt_all, dim)
-        x_2, _ = block_call(1, n_tp, n_cp, o_1, w_o, wo_1, x_1, w_gate, w_up, w_down, gains[1, 1:], gathered=gathered)
-        return x_2, *[a.reshape(PAIR, rows, n_kv, dim) for a in (k_cache, v_cache)]
+        cuts = (96, 48)
+        o_0, k_cache, v_cache, wo_0 = first_call(n_tp, n_cp, hidden, w_q, w_k, w_v, w_o, norm_gain, qk_gain, *angles[0])
+        following = [w_q, w_k, w_v, qk_gain, *angles[1], k_cache, v_cache]
+        x_1, _, q_1, k_all, vt_all, k_cache, v_cache, wo_1 = block_call(0, n_tp, n_cp, *cuts, o_0, w_o, wo_0, hidden, w_gate, w_up, w_down, norm_gain, following=following)
+        o_1, gathered, wo_1 = global_call(n_tp, n_cp, *cuts, q_1, k_all, vt_all, w_o, wo_1, dim)
+        x_2, _ = block_call(1, n_tp, n_cp, *cuts, o_1, w_o, wo_1, x_1, w_gate, w_up, w_down, norm_gain, gathered=gathered)
+        return x_2, k_cache, v_cache
 
     return jax.shard_map(
         device_fn,

time: 782 us -> 739 us (0.945)
  the two profiles are of different devices: /device:TPU:103 before, /device:TPU:97 now
where the time goes in v2:
time: 739 us
  Pallas kernels  722 us (98%)
  local copies, waits for them, and re-layouts  9.76 us (1%)
    pallas_call x2, Pallas kernels, block_call(): pl.pallas_call(functools.partial(block_kernel, layer, n_tp, n_cp, tm, nt,...  545 us
    pallas_call x1, Pallas kernels, first_call(): pl.pallas_call(functools.partial(first_kernel, n_q, n_kv, n_tp, n_cp, 64,...  97.6 us
    pallas_call x1, Pallas kernels, global_call(): pl.pallas_call(functools.partial(global_kernel, groups, n_tp, n_cp, unit,...  79.9 us

profile of v2, /device:TPU:97, one launch (start us, length us, event | category | flops | bytes accessed | tf_op | source)
XLA Modules:
  0.0 738.7 jit_solution(16710873670143231674)
XLA Ops:
  0.6 0.7 convert_element_type.4
  1.3 5.3 multiply_sine_fusion
  6.7 97.6 %first.1 = (bf16[1024,1024]{1,0:T(8,128)(2,1)}, bf16[2,1024,2,256]{3,2,1,0:T(2,128)(2,1)}, bf16[2,1024,2,256]{3,2,1,0:T(2,128)(2,1)}, bf16[4,1024,3840]{2,1,0:T(8,128)(2,1)}) custom-call(bf16[1024,3840]{1,0:T(8,128)(2,1)} %refs_3_.1, bf16[2,3840,512]{2,1,0:T(8,128)(2,1)} %refs_9_.1, bf16[2,3840,512]{2,1,0:T(8,128)(2,1)} %refs_10_.1, ...), custom_call_target="tpu_custom_call" | custom-call | flops 16106127360 | bytes 15728640 | tf_op jit(solution)/shard_map/first/pallas_call | solution.py:307
  104.3 301.9 %block_0.1 = (bf16[1024,3840]{1,0:T(8,128)(2,1)}, bf16[3,1024,1024]{2,1,0:T(8,128)(2,1)}, bf16[1024,1024]{1,0:T(8,128)(2,1)}, bf16[8192,512]{1,0:T(8,128)(2,1)},...) custom-call(bf16[1024,1024]{1,0:T(8,128)(2,1)} %get-tuple-element.18, ...), custom_call_target="tpu_custom_call", output_to_operand_aliasing={{6}: (15, {}), {5}: (14, {})} | custom-call | flops 245618442240 | bytes 479723520 | tf_op jit(solution)/shard_map/block_0/pallas_call | solution.py:1013
  406.2 79.9 %attend_global.1 = (bf16[1024,1024]{1,0:T(8,128)(2,1)}, bf16[3,1024,1024]{2,1,0:T(8,128)(2,1)}, bf16[4,1024,3840]{2,1,0:T(8,128)(2,1)}) custom-call(bf16[1024,1024]{1,0:T(8,128)(2,1)} %get-tuple-element.22.q_ref, bf16[8192,512]{1,0:T(8,128)(2,1)} %get-tuple-element.23.k_hbm, ...), custom_call_target="tpu_custom_call", output_to_operand_aliasing={{2}: (4, {})} | custom-call | flops 17179869184 | bytes 16777216 | tf_op jit(solution)/shard_map/attend_global/pallas_call | solution.py:519
  486.1 242.8 %block_1.1 = (bf16[1024,3840]{1,0:T(8,128)(2,1)}, bf16[3,1024,1024]{2,1,0:T(8,128)(2,1)}) custom-call(bf16[1024,1024]{1,0:T(8,128)(2,1)} %get-tuple-element.26.refs_0_, bf16[2,1024,3840]{2,1,0:T(8,128)(2,1)} %refs_1_.3, bf16[4,1024,3840]{2,1,0:T(8,128)(2,1)} %get-tuple-element.27.refs_2_, ...), custom_call_target="tpu_custom_call", output_to_operand_aliasing={{1}: (8, {})} | custom-call | flops 245618442240 | bytes 479723520 | tf_op jit(solution)/shard_map/block_1/pallas_call | solution.py:1013
  728.9 0.0 copy-start
  728.9 0.0 copy-start.1
  729.0 7.1 copy.25
  736.1 0.0 copy-done
  736.1 1.3 copy.26
  737.4 0.0 copy-done.1
  737.4 1.3 copy.27
  (1 shorter events, 0.0 us)
Async XLA Ops:
  728.9 7.1 copy-start
  728.9 8.4 %copy-start.1 = (bf16[2,1024,2,256]{3,2,1,0:T(2,128)(2,1)S(1)}, bf16[2,1024,2,256]{3,2,1,0:T(2,128)(2,1)}, u32[]{:S(2)}) copy-start(bf16[2,1024,2,256]{3,2,1,0:T(2,128)(2,1)} %get-tuple-element.46) | copy-start | bytes 6291460

commit v3 on v2

--- a/solution.py
+++ b/solution.py
@@ -223,10 +223,6 @@
         g.y_stage(0, g.y_first(PAIR), *map(g.x_first, TWO))
         start(send_kv(1))
 
-    @pl.when(step == q_step + 3)
-    def _():
-        g.x_stage(0)
-
     def project(w_ref, store, finish):
         @pl.loop(0, rows // TILE)
         def _(i):
@@ -263,6 +259,7 @@
         g.y_stage(1)
         g.y_end(0)
         start(g.x_first(PAIR))
+        g.x_stage(0)
         g.x_stage(1)
         g.y_stage(PAIR)
         arrived(*map(send_kv, TWO))
@@ -814,8 +811,10 @@
     served = ready
     if not ready:
         for served in TWO:
-            o_serve(served)
+            arrived(o_first(served))
+            start(o_second(served))
         served = PAIR
+        start(*[o_first(served + t) for t in TWO])
 
     def serve(n, place):
         if served + place < units:

time: 739 us -> 736 us (level)
  no operation moved by 1% of the time
where the time goes in v3:
time: 736 us; the launch traced here: 734 us
  Pallas kernels  718 us (98%)
  local copies, waits for them, and re-layouts  9.76 us (1%)
    pallas_call x2, Pallas kernels, block_call(): pl.pallas_call(functools.partial(block_kernel, layer, n_tp, n_cp, tm, nt,...  540 us
    pallas_call x1, Pallas kernels, first_call(): pl.pallas_call(functools.partial(first_kernel, n_q, n_kv, n_tp, n_cp, 64,...  97.6 us
    pallas_call x1, Pallas kernels, global_call(): pl.pallas_call(functools.partial(global_kernel, groups, n_tp, n_cp, unit,...  79.9 us

profile of v3, /device:TPU:97, one launch (start us, length us, event | category | flops | bytes accessed | tf_op | source)
XLA Modules:
  0.0 734.2 jit_solution(9686297000508120179)
XLA Ops:
  0.6 0.7 convert_element_type.4
  1.3 5.3 multiply_sine_fusion
  6.7 97.6 %first.1 = (bf16[1024,1024]{1,0:T(8,128)(2,1)}, bf16[2,1024,2,256]{3,2,1,0:T(2,128)(2,1)}, bf16[2,1024,2,256]{3,2,1,0:T(2,128)(2,1)}, bf16[4,1024,3840]{2,1,0:T(8,128)(2,1)}) custom-call(bf16[1024,3840]{1,0:T(8,128)(2,1)} %refs_3_.1, bf16[2,3840,512]{2,1,0:T(8,128)(2,1)} %refs_9_.1, bf16[2,3840,512]{2,1,0:T(8,128)(2,1)} %refs_10_.1, ...), custom_call_target="tpu_custom_call" | custom-call | flops 16106127360 | bytes 15728640 | tf_op jit(solution)/shard_map/first/pallas_call | solution.py:304
  104.3 299.2 %block_0.1 = (bf16[1024,3840]{1,0:T(8,128)(2,1)}, bf16[3,1024,1024]{2,1,0:T(8,128)(2,1)}, bf16[1024,1024]{1,0:T(8,128)(2,1)}, bf16[8192,512]{1,0:T(8,128)(2,1)},...) custom-call(bf16[1024,1024]{1,0:T(8,128)(2,1)} %get-tuple-element.18, ...), custom_call_target="tpu_custom_call", output_to_operand_aliasing={{6}: (15, {}), {5}: (14, {})} | custom-call | flops 245618442240 | bytes 479723520 | tf_op jit(solution)/shard_map/block_0/pallas_call | solution.py:1012
  403.5 79.9 %attend_global.1 = (bf16[1024,1024]{1,0:T(8,128)(2,1)}, bf16[3,1024,1024]{2,1,0:T(8,128)(2,1)}, bf16[4,1024,3840]{2,1,0:T(8,128)(2,1)}) custom-call(bf16[1024,1024]{1,0:T(8,128)(2,1)} %get-tuple-element.22.q_ref, bf16[8192,512]{1,0:T(8,128)(2,1)} %get-tuple-element.23.k_hbm, ...), custom_call_target="tpu_custom_call", output_to_operand_aliasing={{2}: (4, {})} | custom-call | flops 17179869184 | bytes 16777216 | tf_op jit(solution)/shard_map/attend_global/pallas_call | solution.py:516
  483.4 241.0 %block_1.1 = (bf16[1024,3840]{1,0:T(8,128)(2,1)}, bf16[3,1024,1024]{2,1,0:T(8,128)(2,1)}) custom-call(bf16[1024,1024]{1,0:T(8,128)(2,1)} %get-tuple-element.26.refs_0_, bf16[2,1024,3840]{2,1,0:T(8,128)(2,1)} %refs_1_.3, bf16[4,1024,3840]{2,1,0:T(8,128)(2,1)} %get-tuple-element.27.refs_2_, ...), custom_call_target="tpu_custom_call", output_to_operand_aliasing={{1}: (8, {})} | custom-call | flops 245618442240 | bytes 479723520 | tf_op jit(solution)/shard_map/block_1/pallas_call | solution.py:1012
  724.4 0.0 copy-start
  724.4 0.0 copy-start.1
  724.4 7.1 copy.25
  731.5 0.0 copy-done
  731.5 1.3 copy.26
  732.9 0.0 copy-done.1
  732.9 1.3 copy.27
  (1 shorter events, 0.0 us)
Async XLA Ops:
  724.4 7.1 copy-start
  724.4 8.4 %copy-start.1 = (bf16[2,1024,2,256]{3,2,1,0:T(2,128)(2,1)S(1)}, bf16[2,1024,2,256]{3,2,1,0:T(2,128)(2,1)}, u32[]{:S(2)}) copy-start(bf16[2,1024,2,256]{3,2,1,0:T(2,128)(2,1)} %get-tuple-element.46) | copy-start | bytes 6291460
